TPU v7x, 512 devices: a whole 4x8x8 slice. The times are simulated.
512 devices in a mesh: lat: 32 (over y, x), lon: 16 (over z, core).
Axes of the slice: x: 4, y: 8, z: 8, core: 2. Of those that a mesh axis runs over, the one named last changes fastest.
Arguments:
- pressure: float32 [1024, 512, 128], P('lat', 'lon'), may hold values from 0.2 to 1.8
- earlier: float32 [1024, 512, 128], P('lat', 'lon'), may hold values from 0.2 to 1.8
- speed_square: float32 [1024, 512, 128], P('lat', 'lon'), may hold values from 0.05 to 0.4
Outputs:
- potential: float32 [1024, 512, 128], P('lat', 'lon')
- pressure_end: float32 [1024, 512, 128], P('lat', 'lon')
All inputs are finite; a program needn't handle non-finite values.
Results may differ from a plain program's by a relative error of at most 0.00002.
Values sent between devices are 32-bit elements; how exact they have to be, the bound alone decides.
No kernel may reach another device: no remote copies, remote signals or barrier semaphores. Data moves between devices by JAX's collectives and lax.ppermute only.
A program may use at most 64 MiB of HBM per device.

v0:
```python
import jax
import jax.numpy as jnp
from jax import lax
from jax.sharding import PartitionSpec as P

STEPS = 4


def padded_2(block, sides, width):
    for axis, dim in sides:
        count = lax.axis_size(axis)
        forward = [(i, i + 1) for i in range(count - 1)]
        backward = [(target, source) for source, target in forward]
        low = lax.ppermute(
            lax.slice_in_dim(block, block.shape[dim] - width, None, axis=dim), axis, forward
        )
        high = lax.ppermute(lax.slice_in_dim(block, 0, width, axis=dim), axis, backward)
        block = jnp.concatenate([low, block, high], axis=dim)
    return block


def copy_for_each(array, axis):
    devices = lax.axis_size(axis)
    return lax.all_to_all(
        jnp.broadcast_to(array[None], (devices, *array.shape)), axis, 0, 0, tiled=True
    )


def combined_pairwise(pieces, combine):
    while len(jax.tree.leaves(pieces)[0]) > 1:
        pieces = jax.vmap(combine)(*(pieces[side::2] for side in (0, 1)))
    return pieces[0]


def carried_in(array, axis, combine, identity):
    devices, here = (lax.axis_size(axis), lax.axis_index(axis))
    passed = jnp.arange(devices) < here

    def kept(part, zero, own):
        part = jnp.where(
            passed.reshape(-1, *(1 for _ in own.shape)), part, jnp.asarray(zero, own.dtype)
        )
        return part

    pieces = copy_for_each(array, axis)
    return combined_pairwise(kept(pieces, identity, array), combine)


def strip_edges(values, dims):
    for dim in dims:
        values = lax.slice_in_dim(values, 1, values.shape[dim] - 1, axis=dim)
    return values


def neighbour(values, dim, start, dims):
    others = [other for other in dims if other != dim]
    values = strip_edges(values, others)
    return lax.slice_in_dim(values, start, start + values.shape[dim] - 2, axis=dim)


def one_step(padded, before, speed_square):
    middle = strip_edges(padded, (0, 1))
    lower = [neighbour(padded, dim, 0, (0, 1)) for dim in (0, 1)]
    upper = [neighbour(padded, dim, 2, (0, 1)) for dim in (0, 1)]
    spread = lower[0] + upper[0] + lower[1] + upper[1] - 4.0 * middle
    return 2.0 * middle - before + speed_square * spread


def on_device(pressure, earlier, speed_square):
    padded = padded_2(pressure, (("lat", 0), ("lon", 1)), STEPS)
    wide_parts = padded_2(
        jnp.concatenate([earlier, speed_square], axis=2), (("lat", 0), ("lon", 1)), STEPS - 1
    )
    wide_earlier, wide_speed_square = jnp.split(wide_parts, 2, axis=2)
    for step in range(STEPS):
        later = one_step(padded, wide_earlier, wide_speed_square)
        values = later
        margin = STEPS - 1 - step
        place = lax.axis_index("lat") * pressure.shape[0] - margin + jnp.arange(values.shape[0])
        keep_cells = (place >= 0) & (place < pressure.shape[0] * lax.axis_size("lat"))
        values = jnp.where(keep_cells.reshape((-1,) + (1,) * 2), values, 0.0)
        place = lax.axis_index("lon") * pressure.shape[1] - margin + jnp.arange(values.shape[1])
        keep_cells = (place >= 0) & (place < pressure.shape[1] * lax.axis_size("lon"))
        values = jnp.where(keep_cells.reshape((-1,) + (1,) * 1), values, 0.0)
        later = values
        before = strip_edges(padded, (0, 1))
        if step < STEPS - 1:
            wide_earlier = strip_edges(before, (0, 1))
            wide_speed_square = strip_edges(wide_speed_square, (0, 1))
        padded = later
    pressure = padded
    here = jnp.cumsum(pressure, axis=0)
    total = lax.slice_in_dim(here, here.shape[0] - 1, here.shape[0], axis=0)

    def add_pair(earlier_total, later_total):
        return earlier_total + later_total

    below = carried_in(total, "lat", add_pair, jnp.zeros_like(total))
    potential = (here + below) / (pressure.shape[0] * lax.axis_size("lat"))
    return (potential, pressure)


def solution(mesh):
    in_specs = (P("lat", "lon", None), P("lat", "lon", None), P("lat", "lon", None))
    out_specs = (P("lat", "lon", None), P("lat", "lon", None))
    return jax.shard_map(
        on_device, mesh=mesh, in_specs=in_specs, out_specs=out_specs, check_vma=False
    )
```

profile of v0, /device:TPU:193, one launch (start us, length us, event | category | flops | bytes accessed | tf_op | source)
XLA Modules:
  0.0 74.9 jit_solution(14001334904242674988)
XLA Ops:
  0.6 1.1 %constant_dynamic-update-slice_fusion.4 = f32[32,32,256]{2,1,0:T(8,128)S(1)} fusion(f32[32,32,128]{2,1,0:T(8,128)} %param.4), kind=kLoop, calls=%fused_computation.54 | loop fusion | bytes 1048576
  1.8 1.1 %constant_dynamic-update-slice_fusion.3 = f32[32,32,256]{2,1,0:T(8,128)S(1)} fusion(f32[32,32,256]{2,1,0:T(8,128)S(1)} %constant_dynamic-update-slice_fusion.4, f32[32,32,128]{2,1,0:T(8,128)} %param.5), kind=kLoop, calls=%fused_computation.53 | loop fusion | bytes 1048576 | tf_op jit(solution)/shard_map/concatenate | solution.py:72
  2.9 3.1 %collective-permute-start.4 = (f32[3,32,256]{2,1,0:T(8,128)S(1)}, f32[3,32,256]{2,1,0:T(8,128)S(1)}, u32[]{:S(2)}, u32[]{:S(2)}) collective-permute-start(f32[3,32,256]{2,1,0:T(8,128)S(1)} %get-tuple-element.4), channel_id=1, source_target_pairs={{0,16},{16,32},{32,48},{48,64},{64,80},{80,96},{96,112},{112,128},... | collective-permute-start | bytes 294920 | tf_op jit(solution)/shard_map/ppermute | solution.py:14
  6.0 1.3 %collective-permute-start.5 = (f32[3,32,256]{2,1,0:T(8,128)S(1)}, f32[3,32,256]{2,1,0:T(8,128)S(1)}, u32[]{:S(2)}, u32[]{:S(2)}) collective-permute-start(f32[3,32,256]{2,1,0:T(8,128)S(1)} %get-tuple-element.5), channel_id=1, source_target_pairs={{16,0},{32,16},{48,32},{64,48},{80,64},{96,80},{112,96},{128,112},... | collective-permute-start | bytes 294920 | tf_op jit(solution)/shard_map/ppermute | solution.py:17
  7.3 4.0 %collective-permute-start = (f32[4,32,128]{2,1,0:T(8,128)S(1)}, f32[4,32,128]{2,1,0:T(8,128)S(1)}, u32[]{:S(2)}, u32[]{:S(2)}) collective-permute-start(f32[4,32,128]{2,1,0:T(8,128)S(1)} %get-tuple-element.9), channel_id=1, source_target_pairs={{0,16},{16,32},{32,48},{48,64},{64,80},{80,96},{96,112},{112,128},... | collective-permute-start | bytes 196616 | tf_op jit(solution)/shard_map/ppermute | solution.py:14
  11.3 1.3 %collective-permute-start.1 = (f32[4,32,128]{2,1,0:T(8,128)S(1)}, f32[4,32,128]{2,1,0:T(8,128)S(1)}, u32[]{:S(2)}, u32[]{:S(2)}) collective-permute-start(f32[4,32,128]{2,1,0:T(8,128)S(1)} %get-tuple-element.8), channel_id=1, source_target_pairs={{16,0},{32,16},{48,32},{64,48},{80,64},{96,80},{112,96},{128,112},... | collective-permute-start | bytes 196616 | tf_op jit(solution)/shard_map/ppermute | solution.py:17
  12.7 0.0 collective-permute-done
  12.8 3.6 %collective-permute-done.1 = f32[4,32,128]{2,1,0:T(8,128)S(1)} collective-permute-done((f32[4,32,128]{2,1,0:T(8,128)S(1)}, f32[4,32,128]{2,1,0:T(8,128)S(1)}, u32[]{:S(2)}, u32[]{:S(2)}) %collective-permute-start.1) | collective-permute-done | bytes 65568 | tf_op jit(solution)/shard_map/ppermute | solution.py:17
  16.4 7.8 %collective-permute-start.2 = (f32[40,4,128]{2,1,0:T(4,128)S(1)}, f32[40,4,128]{2,1,0:T(4,128)S(1)}, u32[]{:S(2)}, u32[]{:S(2)}) collective-permute-start(f32[40,4,128]{2,1,0:T(4,128)S(1)} %get-tuple-element.6), channel_id=1, source_target_pairs={{0,1},{1,2},{2,3},{3,4},{4,5},{5,6},{6,7},{7,8},{8,9},{9,10},{10,1... | collective-permute-start | bytes 245768 | tf_op jit(solution)/shard_map/ppermute | solution.py:14
  24.2 1.9 %collective-permute-start.3 = (f32[40,4,128]{2,1,0:T(4,128)S(1)}, f32[40,4,128]{2,1,0:T(4,128)S(1)}, u32[]{:S(2)}, u32[]{:S(2)}) collective-permute-start(f32[40,4,128]{2,1,0:T(4,128)S(1)} %get-tuple-element.7), channel_id=1, source_target_pairs={{1,0},{2,1},{3,2},{4,3},{5,4},{6,5},{7,6},{8,7},{9,8},{10,9},{11,1... | collective-permute-start | bytes 245768 | tf_op jit(solution)/shard_map/ppermute | solution.py:17
  26.1 0.0 collective-permute-done.4
  26.1 0.0 collective-permute-done.5
  26.1 0.1 pad_maximum_fusion.4
  26.2 4.9 %collective-permute-start.6 = (f32[38,3,256]{2,1,0:T(4,128)S(1)}, f32[38,3,256]{2,1,0:T(4,128)S(1)}, u32[]{:S(2)}, u32[]{:S(2)}) collective-permute-start(f32[38,3,256]{2,1,0:T(4,128)S(1)} %get-tuple-element.2), channel_id=1, source_target_pairs={{0,1},{1,2},{2,3},{3,4},{4,5},{5,6},{6,7},{7,8},{8,9},{9,10},{10,1... | collective-permute-start | bytes 350216 | tf_op jit(solution)/shard_map/ppermute | solution.py:14
  31.0 1.9 %collective-permute-start.7 = (f32[38,3,256]{2,1,0:T(4,128)S(1)}, f32[38,3,256]{2,1,0:T(4,128)S(1)}, u32[]{:S(2)}, u32[]{:S(2)}) collective-permute-start(f32[38,3,256]{2,1,0:T(4,128)S(1)} %get-tuple-element.3), channel_id=1, source_target_pairs={{1,0},{2,1},{3,2},{4,3},{5,4},{6,5},{7,6},{8,7},{9,8},{10,9},{11,1... | collective-permute-start | bytes 350216 | tf_op jit(solution)/shard_map/ppermute | solution.py:17
  33.0 0.1 pad_maximum_fusion.1
  33.1 0.1 collective-permute-done.6
  33.2 5.6 %collective-permute-done.7 = f32[38,3,256]{2,1,0:T(4,128)S(1)} collective-permute-done((f32[38,3,256]{2,1,0:T(4,128)S(1)}, f32[38,3,256]{2,1,0:T(4,128)S(1)}, u32[]{:S(2)}, u32[]{:S(2)}) %collective-permute-start.7) | collective-permute-done | bytes 116768 | tf_op jit(solution)/shard_map/ppermute | solution.py:17
  38.8 0.2 pad_maximum_fusion
  39.0 0.4 fusion.4
  39.4 0.5 fusion.9
  40.0 0.0 copy-start
  40.0 0.5 fusion.14
  40.5 0.5 copy-done
  41.0 0.3 fusion.19
  41.3 0.0 copy-start.1
  41.4 2.0 %fusion.24 = f32[32,32,128]{2,1,0:T(8,128)S(1)} fusion(f32[32,32,128]{2,1,0:T(8,128)S(1)} %fusion.19), kind=kOutput, calls=%fused_computation.67 | output fusion | flops 4063232 | bytes 1048576 | tf_op jit(solution)/shard_map/jit(cumsum)/reduce_window_sum | solution.py:92
  43.4 0.9 %broadcast_in_dim.123 = f32[32,1,32,128]{3,2,1,0:T(8,128)} broadcast(f32[32,128]{1,0:T(8,128)S(1)} %slice_bitcast_fusion), dimensions={2,3} | broadcast | bytes 540672 | tf_op jit(solution)/shard_map/broadcast_in_dim | solution.py:25
  44.2 15.0 %all-to-all-start = ((f32[32,1,32,128]{3,2,1,0:T(8,128)}), f32[32,1,32,128]{3,2,1,0:T(8,128)S(1)}, u32[]{:S(2)}, u32[]{:S(2)}) async-start(f32[32,1,32,128]{3,2,1,0:T(8,128)} %broadcast_in_dim.123), calls=%async_computation | async-start | bytes 1048576 | tf_op jit(solution)/shard_map/all_to_all | solution.py:24
  59.3 14.6 %all-to-all-done = f32[32,1,32,128]{3,2,1,0:T(8,128)S(1)} async-done(((f32[32,1,32,128]{3,2,1,0:T(8,128)}), f32[32,1,32,128]{3,2,1,0:T(8,128)S(1)}, u32[]{:S(2)}, u32[]{:S(2)}) %all-to-all-start) | async-done | bytes 524320 | tf_op jit(solution)/shard_map/all_to_all | solution.py:24
  73.8 0.1 broadcast_select_fusion
  74.1 0.9 %add_multiply_fusion = f32[32,32,128]{2,1,0:T(8,128)} fusion(f32[32,32,128]{2,1,0:T(8,128)S(1)} %fusion.24, f32[32,128]{1,0:T(8,128)S(1)} %fusion.20), kind=kLoop, calls=%fused_computation.38 | loop fusion | flops 262144 | bytes 1064960 | tf_op jit(solution)/shard_map/div | solution.py:99
  (22 shorter events, 0.3 us)
Async XLA Ops:
  0.6 6.7 %copy-start.2 = (f32[32,32,128]{2,1,0:T(8,128)S(1)}, f32[32,32,128]{2,1,0:T(8,128)}, u32[]{:S(2)}) copy-start(f32[32,32,128]{2,1,0:T(8,128)} %param.3) | copy-start | bytes 1572868
  2.9 23.2 %collective-permute-start.4 = (f32[3,32,256]{2,1,0:T(8,128)S(1)}, f32[3,32,256]{2,1,0:T(8,128)S(1)}, u32[]{:S(2)}, u32[]{:S(2)}) collective-permute-start(f32[3,32,256]{2,1,0:T(8,128)S(1)} %get-tuple-element.4), channel_id=1, source_target_pairs={{0,16},{16,32},{32,48},{48,64},{64,80},{80,96},{96,112},{112,128},... | collective-permute-start | bytes 294920 | tf_op jit(solution)/shard_map/ppermute | solution.py:14
  6.0 20.1 %collective-permute-start.5 = (f32[3,32,256]{2,1,0:T(8,128)S(1)}, f32[3,32,256]{2,1,0:T(8,128)S(1)}, u32[]{:S(2)}, u32[]{:S(2)}) collective-permute-start(f32[3,32,256]{2,1,0:T(8,128)S(1)} %get-tuple-element.5), channel_id=1, source_target_pairs={{16,0},{32,16},{48,32},{64,48},{80,64},{96,80},{112,96},{128,112},... | collective-permute-start | bytes 294920 | tf_op jit(solution)/shard_map/ppermute | solution.py:17
  7.3 5.4 %collective-permute-start = (f32[4,32,128]{2,1,0:T(8,128)S(1)}, f32[4,32,128]{2,1,0:T(8,128)S(1)}, u32[]{:S(2)}, u32[]{:S(2)}) collective-permute-start(f32[4,32,128]{2,1,0:T(8,128)S(1)} %get-tuple-element.9), channel_id=1, source_target_pairs={{0,16},{16,32},{32,48},{48,64},{64,80},{80,96},{96,112},{112,128},... | collective-permute-start | bytes 196616 | tf_op jit(solution)/shard_map/ppermute | solution.py:14
  11.3 5.0 %collective-permute-start.1 = (f32[4,32,128]{2,1,0:T(8,128)S(1)}, f32[4,32,128]{2,1,0:T(8,128)S(1)}, u32[]{:S(2)}, u32[]{:S(2)}) collective-permute-start(f32[4,32,128]{2,1,0:T(8,128)S(1)} %get-tuple-element.8), channel_id=1, source_target_pairs={{16,0},{32,16},{48,32},{64,48},{80,64},{96,80},{112,96},{128,112},... | collective-permute-start | bytes 196616 | tf_op jit(solution)/shard_map/ppermute | solution.py:17
  16.4 16.6 %collective-permute-start.2 = (f32[40,4,128]{2,1,0:T(4,128)S(1)}, f32[40,4,128]{2,1,0:T(4,128)S(1)}, u32[]{:S(2)}, u32[]{:S(2)}) collective-permute-start(f32[40,4,128]{2,1,0:T(4,128)S(1)} %get-tuple-element.6), channel_id=1, source_target_pairs={{0,1},{1,2},{2,3},{3,4},{4,5},{5,6},{6,7},{7,8},{8,9},{9,10},{10,1... | collective-permute-start | bytes 245768 | tf_op jit(solution)/shard_map/ppermute | solution.py:14
  24.2 8.8 %collective-permute-start.3 = (f32[40,4,128]{2,1,0:T(4,128)S(1)}, f32[40,4,128]{2,1,0:T(4,128)S(1)}, u32[]{:S(2)}, u32[]{:S(2)}) collective-permute-start(f32[40,4,128]{2,1,0:T(4,128)S(1)} %get-tuple-element.7), channel_id=1, source_target_pairs={{1,0},{2,1},{3,2},{4,3},{5,4},{6,5},{7,6},{8,7},{9,8},{10,9},{11,1... | collective-permute-start | bytes 245768 | tf_op jit(solution)/shard_map/ppermute | solution.py:17
  26.2 7.0 %collective-permute-start.6 = (f32[38,3,256]{2,1,0:T(4,128)S(1)}, f32[38,3,256]{2,1,0:T(4,128)S(1)}, u32[]{:S(2)}, u32[]{:S(2)}) collective-permute-start(f32[38,3,256]{2,1,0:T(4,128)S(1)} %get-tuple-element.2), channel_id=1, source_target_pairs={{0,1},{1,2},{2,3},{3,4},{4,5},{5,6},{6,7},{7,8},{8,9},{9,10},{10,1... | collective-permute-start | bytes 350216 | tf_op jit(solution)/shard_map/ppermute | solution.py:14
  31.0 7.8 %collective-permute-start.7 = (f32[38,3,256]{2,1,0:T(4,128)S(1)}, f32[38,3,256]{2,1,0:T(4,128)S(1)}, u32[]{:S(2)}, u32[]{:S(2)}) collective-permute-start(f32[38,3,256]{2,1,0:T(4,128)S(1)} %get-tuple-element.3), channel_id=1, source_target_pairs={{1,0},{2,1},{3,2},{4,3},{5,4},{6,5},{7,6},{8,7},{9,8},{10,9},{11,1... | collective-permute-start | bytes 350216 | tf_op jit(solution)/shard_map/ppermute | solution.py:17
  40.0 1.0 %copy-start = (f32[32,32,128]{2,1,0:T(8,128)S(1)}, f32[32,32,128]{2,1,0:T(8,128)}, u32[]{:S(2)}) copy-start(f32[32,32,128]{2,1,0:T(8,128)} %param.5) | copy-start | bytes 1572868
  41.3 32.6 %copy-start.1 = (f32[32,32,128]{2,1,0:T(8,128)}, f32[32,32,128]{2,1,0:T(8,128)S(1)}, u32[]{:S(2)}) copy-start(f32[32,32,128]{2,1,0:T(8,128)S(1)} %fusion.19) | copy-start | bytes 1572868
  44.2 29.6 %all-to-all-start = ((f32[32,1,32,128]{3,2,1,0:T(8,128)}), f32[32,1,32,128]{3,2,1,0:T(8,128)S(1)}, u32[]{:S(2)}, u32[]{:S(2)}) async-start(f32[32,1,32,128]{3,2,1,0:T(8,128)} %broadcast_in_dim.123), calls=%async_computation | async-start | bytes 1048576 | tf_op jit(solution)/shard_map/all_to_all | solution.py:24
where the time goes:
time: 75.4 us; the launch traced here: 74.9 us
  starting transfers between devices  41.2 us (55%)
  waiting for transfers between devices  23.8 us (32%)
  other arithmetic  5.21 us (7%)
  local copies, waits for them, and re-layouts  3.74 us (5%)
  between operations  0.97 us (1%)
    ppermute x4, starting transfers between devices, padded_2(): lax.ppermute(lax.slice_in_dim(block, block.shape[dim] - width, None, axis...  19.7 us
    all_to_all x1, starting transfers between devices, copy_for_each(): lax.all_to_all(jnp.broadcast_to(array[None], (devices, *array.shape)), ax...  15 us
    all_to_all x1, waiting for transfers between devices, copy_for_each(): lax.all_to_all(jnp.broadcast_to(array[None], (devices, *array.shape)), ax...  14.6 us
    ppermute x4, waiting for transfers between devices, padded_2(): lax.ppermute(lax.slice_in_dim(block, 0, width, axis=dim), axis, backward)  9.18 us
    ppermute x4, starting transfers between devices, padded_2(): lax.ppermute(lax.slice_in_dim(block, 0, width, axis=dim), axis, backward)  6.43 us
    another operation x1, other arithmetic, on_device(): here = jnp.cumsum(pressure, axis=0)  2 us
    select_n x4, other arithmetic, on_device(): values = jnp.where(keep_cells.reshape((-1,) + (1,) * 1), values, 0.0)  1.75 us
    unnamed x9, local copies, waits for them, and re-layouts  1.74 us
  transfers between devices with their start and end apart: 9, of which 4 were waited for; matrix products, arithmetic and copies ran while one was open for 0% of the time, Pallas kernels for 0%

commit v1 on v0

v1 whole, which is shorter than its diff:
```python
import jax
import jax.numpy as jnp
from jax import lax
from jax.sharding import Mesh, PartitionSpec as P

STEPS = 4
LAT = ("y", "x")
LON = ("z", "core")


def padded_2(block, sides, width):
    for axis, dim in sides:
        count = lax.axis_size(axis)
        forward = [(i, i + 1) for i in range(count - 1)]
        backward = [(target, source) for source, target in forward]
        low = lax.ppermute(
            lax.slice_in_dim(block, block.shape[dim] - width, None, axis=dim), axis, forward
        )
        high = lax.ppermute(lax.slice_in_dim(block, 0, width, axis=dim), axis, backward)
        block = jnp.concatenate([low, block, high], axis=dim)
    return block


def all_of(array, axis):
    devices = lax.axis_size(axis)
    copies = jnp.broadcast_to(array, (devices, *array.shape[1:]))
    return lax.all_to_all(copies, axis, 0, 0, tiled=True)


def before(pieces, axis):
    passed = jnp.arange(pieces.shape[0]) < lax.axis_index(axis)
    return jnp.sum(jnp.where(passed.reshape(-1, 1, 1), pieces, 0.0), axis=0, keepdims=True)


def carried_in(total):
    row = all_of(total, "x")
    rows = all_of(jnp.sum(row, axis=0, keepdims=True), "y")
    return before(row, "x") + before(rows, "y")


def strip_edges(values, dims):
    for dim in dims:
        values = lax.slice_in_dim(values, 1, values.shape[dim] - 1, axis=dim)
    return values


def neighbour(values, dim, start, dims):
    others = [other for other in dims if other != dim]
    values = strip_edges(values, others)
    return lax.slice_in_dim(values, start, start + values.shape[dim] - 2, axis=dim)


def one_step(padded, before, speed_square):
    middle = strip_edges(padded, (0, 1))
    lower = [neighbour(padded, dim, 0, (0, 1)) for dim in (0, 1)]
    upper = [neighbour(padded, dim, 2, (0, 1)) for dim in (0, 1)]
    spread = lower[0] + upper[0] + lower[1] + upper[1] - 4.0 * middle
    return 2.0 * middle - before + speed_square * spread


def on_device(pressure, earlier, speed_square):
    padded = padded_2(pressure, ((LAT, 0), (LON, 1)), STEPS)
    wide_parts = padded_2(
        jnp.concatenate([earlier, speed_square], axis=2), ((LAT, 0), (LON, 1)), STEPS - 1
    )
    wide_earlier, wide_speed_square = jnp.split(wide_parts, 2, axis=2)
    for step in range(STEPS):
        later = one_step(padded, wide_earlier, wide_speed_square)
        values = later
        margin = STEPS - 1 - step
        place = lax.axis_index(LAT) * pressure.shape[0] - margin + jnp.arange(values.shape[0])
        keep_cells = (place >= 0) & (place < pressure.shape[0] * lax.axis_size(LAT))
        values = jnp.where(keep_cells.reshape((-1,) + (1,) * 2), values, 0.0)
        place = lax.axis_index(LON) * pressure.shape[1] - margin + jnp.arange(values.shape[1])
        keep_cells = (place >= 0) & (place < pressure.shape[1] * lax.axis_size(LON))
        values = jnp.where(keep_cells.reshape((-1,) + (1,) * 1), values, 0.0)
        later = values
        before = strip_edges(padded, (0, 1))
        if step < STEPS - 1:
            wide_earlier = strip_edges(before, (0, 1))
            wide_speed_square = strip_edges(wide_speed_square, (0, 1))
        padded = later
    pressure = padded
    here = jnp.cumsum(pressure, axis=0)
    total = lax.slice_in_dim(here, here.shape[0] - 1, here.shape[0], axis=0)

    below = carried_in(total)
    potential = (here + below) / (pressure.shape[0] * lax.axis_size(LAT))
    return (potential, pressure)


def solution(mesh):
    fine = Mesh(mesh.devices.reshape(8, 4, 8, 2), ("y", "x", "z", "core"))
    spec = P(LAT, LON, None)
    return jax.shard_map(
        on_device, mesh=fine, in_specs=(spec,) * 3, out_specs=(spec,) * 2, check_vma=False
    )
```

time: 75.4 us -> 74.9 us (level)
  waiting for transfers between devices: 23.8 us -> 21.7 us
  starting transfers between devices: 41.2 us -> 42.3 us
    all_to_all x1 -> x2, waiting for transfers between devices: 14.6 us -> 12.4 us  [all_of(): return lax.all_to_all(copies, axis, 0, 0, tiled=True)]
    all_to_all x1 -> x2, starting transfers between devices: 15 us -> 16.2 us  [all_of(): return lax.all_to_all(copies, axis, 0, 0, tiled=True)]
  transfers between devices with their start and end apart: 9 -> 10, of which waited for: 4 -> 5; matrix products, arithmetic and copies ran while one was open for 0% -> 0% of each run, Pallas kernels for 0% -> 0%
where the time goes in v1:
time: 74.9 us; the launch traced here: 74.3 us
  starting transfers between devices  42.3 us (56%)
  waiting for transfers between devices  21.7 us (29%)
  other arithmetic  5.19 us (7%)
  local copies, waits for them, and re-layouts  4.18 us (6%)
  between operations  0.93 us (1%)
    ppermute x4, starting transfers between devices, padded_2(): lax.ppermute(lax.slice_in_dim(block, block.shape[dim] - width, None, axis...  19.7 us
    all_to_all x2, starting transfers between devices, all_of(): return lax.all_to_all(copies, axis, 0, 0, tiled=True)  16.2 us
    all_to_all x2, waiting for transfers between devices, all_of(): return lax.all_to_all(copies, axis, 0, 0, tiled=True)  12.4 us
    ppermute x4, waiting for transfers between devices, padded_2(): lax.ppermute(lax.slice_in_dim(block, 0, width, axis=dim), axis, backward)  9.17 us
    ppermute x4, starting transfers between devices, padded_2(): lax.ppermute(lax.slice_in_dim(block, 0, width, axis=dim), axis, backward)  6.43 us
    another operation x1, other arithmetic, on_device(): here = jnp.cumsum(pressure, axis=0)  2 us
    select_n x4, other arithmetic, on_device(): values = jnp.where(keep_cells.reshape((-1,) + (1,) * 1), values, 0.0)  1.75 us
    unnamed x9, local copies, waits for them, and re-layouts  1.74 us
  transfers between devices with their start and end apart: 10, of which 5 were waited for; matrix products, arithmetic and copies ran while one was open for 0% of the time, Pallas kernels for 0%

profile of v1, /device:TPU:193, one launch (start us, length us, event | category | flops | bytes accessed | tf_op | source)
XLA Modules:
  0.0 74.3 jit_solution(3055834926812505338)
XLA Ops:
  0.6 1.1 %constant_dynamic-update-slice_fusion.4 = f32[32,32,256]{2,1,0:T(8,128)S(1)} fusion(f32[32,32,128]{2,1,0:T(8,128)} %param.4), kind=kLoop, calls=%fused_computation.49 | loop fusion | bytes 1048576
  1.8 1.1 %constant_dynamic-update-slice_fusion.3 = f32[32,32,256]{2,1,0:T(8,128)S(1)} fusion(f32[32,32,256]{2,1,0:T(8,128)S(1)} %constant_dynamic-update-slice_fusion.4, f32[32,32,128]{2,1,0:T(8,128)} %param.5), kind=kLoop, calls=%fused_computation.48 | loop fusion | bytes 1048576 | tf_op jit(solution)/shard_map/concatenate | solution.py:64
  2.9 3.1 %collective-permute-start.4 = (f32[3,32,256]{2,1,0:T(8,128)S(1)}, f32[3,32,256]{2,1,0:T(8,128)S(1)}, u32[]{:S(2)}, u32[]{:S(2)}) collective-permute-start(f32[3,32,256]{2,1,0:T(8,128)S(1)} %get-tuple-element.6), channel_id=1, source_target_pairs={{0,16},{16,32},{32,48},{48,64},{64,80},{80,96},{96,112},{112,128},... | collective-permute-start | bytes 294920 | tf_op jit(solution)/shard_map/ppermute | solution.py:16
  6.0 1.3 %collective-permute-start.5 = (f32[3,32,256]{2,1,0:T(8,128)S(1)}, f32[3,32,256]{2,1,0:T(8,128)S(1)}, u32[]{:S(2)}, u32[]{:S(2)}) collective-permute-start(f32[3,32,256]{2,1,0:T(8,128)S(1)} %get-tuple-element.7), channel_id=1, source_target_pairs={{16,0},{32,16},{48,32},{64,48},{80,64},{96,80},{112,96},{128,112},... | collective-permute-start | bytes 294920 | tf_op jit(solution)/shard_map/ppermute | solution.py:19
  7.3 4.0 %collective-permute-start = (f32[4,32,128]{2,1,0:T(8,128)S(1)}, f32[4,32,128]{2,1,0:T(8,128)S(1)}, u32[]{:S(2)}, u32[]{:S(2)}) collective-permute-start(f32[4,32,128]{2,1,0:T(8,128)S(1)} %get-tuple-element.11), channel_id=1, source_target_pairs={{0,16},{16,32},{32,48},{48,64},{64,80},{80,96},{96,112},{112,128},... | collective-permute-start | bytes 196616 | tf_op jit(solution)/shard_map/ppermute | solution.py:16
  11.3 1.3 %collective-permute-start.1 = (f32[4,32,128]{2,1,0:T(8,128)S(1)}, f32[4,32,128]{2,1,0:T(8,128)S(1)}, u32[]{:S(2)}, u32[]{:S(2)}) collective-permute-start(f32[4,32,128]{2,1,0:T(8,128)S(1)} %get-tuple-element.10), channel_id=1, source_target_pairs={{16,0},{32,16},{48,32},{64,48},{80,64},{96,80},{112,96},{128,112},... | collective-permute-start | bytes 196616 | tf_op jit(solution)/shard_map/ppermute | solution.py:19
  12.8 3.6 %collective-permute-done.1 = f32[4,32,128]{2,1,0:T(8,128)S(1)} collective-permute-done((f32[4,32,128]{2,1,0:T(8,128)S(1)}, f32[4,32,128]{2,1,0:T(8,128)S(1)}, u32[]{:S(2)}, u32[]{:S(2)}) %collective-permute-start.1) | collective-permute-done | bytes 65568 | tf_op jit(solution)/shard_map/ppermute | solution.py:19
  16.4 7.8 %collective-permute-start.2 = (f32[40,4,128]{2,1,0:T(4,128)S(1)}, f32[40,4,128]{2,1,0:T(4,128)S(1)}, u32[]{:S(2)}, u32[]{:S(2)}) collective-permute-start(f32[40,4,128]{2,1,0:T(4,128)S(1)} %get-tuple-element.8), channel_id=1, source_target_pairs={{0,1},{1,2},{2,3},{3,4},{4,5},{5,6},{6,7},{7,8},{8,9},{9,10},{10,1... | collective-permute-start | bytes 245768 | tf_op jit(solution)/shard_map/ppermute | solution.py:16
  24.2 1.9 %collective-permute-start.3 = (f32[40,4,128]{2,1,0:T(4,128)S(1)}, f32[40,4,128]{2,1,0:T(4,128)S(1)}, u32[]{:S(2)}, u32[]{:S(2)}) collective-permute-start(f32[40,4,128]{2,1,0:T(4,128)S(1)} %get-tuple-element.9), channel_id=1, source_target_pairs={{1,0},{2,1},{3,2},{4,3},{5,4},{6,5},{7,6},{8,7},{9,8},{10,9},{11,1... | collective-permute-start | bytes 245768 | tf_op jit(solution)/shard_map/ppermute | solution.py:19
  26.1 0.1 pad_maximum_fusion.4
  26.2 4.9 %collective-permute-start.6 = (f32[38,3,256]{2,1,0:T(4,128)S(1)}, f32[38,3,256]{2,1,0:T(4,128)S(1)}, u32[]{:S(2)}, u32[]{:S(2)}) collective-permute-start(f32[38,3,256]{2,1,0:T(4,128)S(1)} %get-tuple-element.4), channel_id=1, source_target_pairs={{0,1},{1,2},{2,3},{3,4},{4,5},{5,6},{6,7},{7,8},{8,9},{9,10},{10,1... | collective-permute-start | bytes 350216 | tf_op jit(solution)/shard_map/ppermute | solution.py:16
  31.0 1.9 %collective-permute-start.7 = (f32[38,3,256]{2,1,0:T(4,128)S(1)}, f32[38,3,256]{2,1,0:T(4,128)S(1)}, u32[]{:S(2)}, u32[]{:S(2)}) collective-permute-start(f32[38,3,256]{2,1,0:T(4,128)S(1)} %get-tuple-element.5), channel_id=1, source_target_pairs={{1,0},{2,1},{3,2},{4,3},{5,4},{6,5},{7,6},{8,7},{9,8},{10,9},{11,1... | collective-permute-start | bytes 350216 | tf_op jit(solution)/shard_map/ppermute | solution.py:19
  33.0 0.1 pad_maximum_fusion.1
  33.1 0.1 collective-permute-done.6
  33.2 5.6 %collective-permute-done.7 = f32[38,3,256]{2,1,0:T(4,128)S(1)} collective-permute-done((f32[38,3,256]{2,1,0:T(4,128)S(1)}, f32[38,3,256]{2,1,0:T(4,128)S(1)}, u32[]{:S(2)}, u32[]{:S(2)}) %collective-permute-start.7) | collective-permute-done | bytes 116768 | tf_op jit(solution)/shard_map/ppermute | solution.py:19
  38.8 0.2 pad_maximum_fusion
  39.0 0.4 fusion.4
  39.4 0.5 fusion.9
  40.0 0.5 fusion.14
  40.5 0.5 copy-done
  41.0 0.3 fusion.19
  41.3 0.0 copy-start.1
  41.4 2.0 %fusion.24 = f32[32,32,128]{2,1,0:T(8,128)S(1)} fusion(f32[32,32,128]{2,1,0:T(8,128)S(1)} %fusion.19), kind=kOutput, calls=%fused_computation.64 | output fusion | flops 4063232 | bytes 1048576 | tf_op jit(solution)/shard_map/jit(cumsum)/reduce_window_sum | solution.py:84
  43.4 0.6 broadcast_in_dim.141
  44.0 8.0 %all-to-all-start = ((f32[4,32,128]{2,1,0:T(8,128)}), f32[4,32,128]{2,1,0:T(8,128)S(1)}, u32[]{:S(2)}, u32[]{:S(2)}) async-start(f32[4,32,128]{2,1,0:T(8,128)} %broadcast_in_dim.141), calls=%async_computation | async-start | bytes 131072 | tf_op jit(solution)/shard_map/all_to_all | solution.py:27
  52.0 4.5 %all-to-all-done = f32[4,32,128]{2,1,0:T(8,128)S(1)} async-done(((f32[4,32,128]{2,1,0:T(8,128)}), f32[4,32,128]{2,1,0:T(8,128)S(1)}, u32[]{:S(2)}, u32[]{:S(2)}) %all-to-all-start) | async-done | bytes 65568 | tf_op jit(solution)/shard_map/all_to_all | solution.py:27
  56.5 0.1 fusion.20
  56.5 0.7 broadcast_in_dim.144
  57.2 8.2 %all-to-all-start.1 = ((f32[8,32,128]{2,1,0:T(8,128)}), f32[8,32,128]{2,1,0:T(8,128)S(1)}, u32[]{:S(2)}, u32[]{:S(2)}) async-start(f32[8,32,128]{2,1,0:T(8,128)} %broadcast_in_dim.144), calls=%async_computation.1 | async-start | bytes 262144 | tf_op jit(solution)/shard_map/all_to_all | solution.py:27
  65.4 7.9 %all-to-all-done.1 = f32[8,32,128]{2,1,0:T(8,128)S(1)} async-done(((f32[8,32,128]{2,1,0:T(8,128)}), f32[8,32,128]{2,1,0:T(8,128)S(1)}, u32[]{:S(2)}, u32[]{:S(2)}) %all-to-all-start.1) | async-done | bytes 131104 | tf_op jit(solution)/shard_map/all_to_all | solution.py:27
  73.4 0.1 select_reduce_fusion
  73.5 0.9 %add_multiply_fusion = f32[32,32,128]{2,1,0:T(8,128)} fusion(f32[32,32,128]{2,1,0:T(8,128)S(1)} %fusion.24, f32[32,128]{1,0:T(8,128)S(1)} %add.180), kind=kLoop, calls=%fused_computation.38 | loop fusion | flops 262144 | bytes 1064960 | tf_op jit(solution)/shard_map/div | solution.py:88
  (23 shorter events, 0.2 us)
Async XLA Ops:
  0.6 6.7 %copy-start.2 = (f32[32,32,128]{2,1,0:T(8,128)S(1)}, f32[32,32,128]{2,1,0:T(8,128)}, u32[]{:S(2)}) copy-start(f32[32,32,128]{2,1,0:T(8,128)} %param.3) | copy-start | bytes 1572868
  2.9 23.2 %collective-permute-start.4 = (f32[3,32,256]{2,1,0:T(8,128)S(1)}, f32[3,32,256]{2,1,0:T(8,128)S(1)}, u32[]{:S(2)}, u32[]{:S(2)}) collective-permute-start(f32[3,32,256]{2,1,0:T(8,128)S(1)} %get-tuple-element.6), channel_id=1, source_target_pairs={{0,16},{16,32},{32,48},{48,64},{64,80},{80,96},{96,112},{112,128},... | collective-permute-start | bytes 294920 | tf_op jit(solution)/shard_map/ppermute | solution.py:16
  6.0 20.1 %collective-permute-start.5 = (f32[3,32,256]{2,1,0:T(8,128)S(1)}, f32[3,32,256]{2,1,0:T(8,128)S(1)}, u32[]{:S(2)}, u32[]{:S(2)}) collective-permute-start(f32[3,32,256]{2,1,0:T(8,128)S(1)} %get-tuple-element.7), channel_id=1, source_target_pairs={{16,0},{32,16},{48,32},{64,48},{80,64},{96,80},{112,96},{128,112},... | collective-permute-start | bytes 294920 | tf_op jit(solution)/shard_map/ppermute | solution.py:19
  7.3 5.4 %collective-permute-start = (f32[4,32,128]{2,1,0:T(8,128)S(1)}, f32[4,32,128]{2,1,0:T(8,128)S(1)}, u32[]{:S(2)}, u32[]{:S(2)}) collective-permute-start(f32[4,32,128]{2,1,0:T(8,128)S(1)} %get-tuple-element.11), channel_id=1, source_target_pairs={{0,16},{16,32},{32,48},{48,64},{64,80},{80,96},{96,112},{112,128},... | collective-permute-start | bytes 196616 | tf_op jit(solution)/shard_map/ppermute | solution.py:16
  11.3 5.0 %collective-permute-start.1 = (f32[4,32,128]{2,1,0:T(8,128)S(1)}, f32[4,32,128]{2,1,0:T(8,128)S(1)}, u32[]{:S(2)}, u32[]{:S(2)}) collective-permute-start(f32[4,32,128]{2,1,0:T(8,128)S(1)} %get-tuple-element.10), channel_id=1, source_target_pairs={{16,0},{32,16},{48,32},{64,48},{80,64},{96,80},{112,96},{128,112},... | collective-permute-start | bytes 196616 | tf_op jit(solution)/shard_map/ppermute | solution.py:19
  16.4 16.6 %collective-permute-start.2 = (f32[40,4,128]{2,1,0:T(4,128)S(1)}, f32[40,4,128]{2,1,0:T(4,128)S(1)}, u32[]{:S(2)}, u32[]{:S(2)}) collective-permute-start(f32[40,4,128]{2,1,0:T(4,128)S(1)} %get-tuple-element.8), channel_id=1, source_target_pairs={{0,1},{1,2},{2,3},{3,4},{4,5},{5,6},{6,7},{7,8},{8,9},{9,10},{10,1... | collective-permute-start | bytes 245768 | tf_op jit(solution)/shard_map/ppermute | solution.py:16
  24.2 8.8 %collective-permute-start.3 = (f32[40,4,128]{2,1,0:T(4,128)S(1)}, f32[40,4,128]{2,1,0:T(4,128)S(1)}, u32[]{:S(2)}, u32[]{:S(2)}) collective-permute-start(f32[40,4,128]{2,1,0:T(4,128)S(1)} %get-tuple-element.9), channel_id=1, source_target_pairs={{1,0},{2,1},{3,2},{4,3},{5,4},{6,5},{7,6},{8,7},{9,8},{10,9},{11,1... | collective-permute-start | bytes 245768 | tf_op jit(solution)/shard_map/ppermute | solution.py:19
  26.2 7.0 %collective-permute-start.6 = (f32[38,3,256]{2,1,0:T(4,128)S(1)}, f32[38,3,256]{2,1,0:T(4,128)S(1)}, u32[]{:S(2)}, u32[]{:S(2)}) collective-permute-start(f32[38,3,256]{2,1,0:T(4,128)S(1)} %get-tuple-element.4), channel_id=1, source_target_pairs={{0,1},{1,2},{2,3},{3,4},{4,5},{5,6},{6,7},{7,8},{8,9},{9,10},{10,1... | collective-permute-start | bytes 350216 | tf_op jit(solution)/shard_map/ppermute | solution.py:16
  31.0 7.8 %collective-permute-start.7 = (f32[38,3,256]{2,1,0:T(4,128)S(1)}, f32[38,3,256]{2,1,0:T(4,128)S(1)}, u32[]{:S(2)}, u32[]{:S(2)}) collective-permute-start(f32[38,3,256]{2,1,0:T(4,128)S(1)} %get-tuple-element.5), channel_id=1, source_target_pairs={{1,0},{2,1},{3,2},{4,3},{5,4},{6,5},{7,6},{8,7},{9,8},{10,9},{11,1... | collective-permute-start | bytes 350216 | tf_op jit(solution)/shard_map/ppermute | solution.py:19
  40.0 1.0 %copy-start = (f32[32,32,128]{2,1,0:T(8,128)S(1)}, f32[32,32,128]{2,1,0:T(8,128)}, u32[]{:S(2)}) copy-start(f32[32,32,128]{2,1,0:T(8,128)} %param.5) | copy-start | bytes 1572868
  41.3 33.0 %copy-start.1 = (f32[32,32,128]{2,1,0:T(8,128)}, f32[32,32,128]{2,1,0:T(8,128)S(1)}, u32[]{:S(2)}) copy-start(f32[32,32,128]{2,1,0:T(8,128)S(1)} %fusion.19) | copy-start | bytes 1572868
  44.0 12.4 %all-to-all-start = ((f32[4,32,128]{2,1,0:T(8,128)}), f32[4,32,128]{2,1,0:T(8,128)S(1)}, u32[]{:S(2)}, u32[]{:S(2)}) async-start(f32[4,32,128]{2,1,0:T(8,128)} %broadcast_in_dim.141), calls=%async_computation | async-start | bytes 131072 | tf_op jit(solution)/shard_map/all_to_all | solution.py:27
  57.2 16.2 %all-to-all-start.1 = ((f32[8,32,128]{2,1,0:T(8,128)}), f32[8,32,128]{2,1,0:T(8,128)S(1)}, u32[]{:S(2)}, u32[]{:S(2)}) async-start(f32[8,32,128]{2,1,0:T(8,128)} %broadcast_in_dim.144), calls=%async_computation.1 | async-start | bytes 262144 | tf_op jit(solution)/shard_map/all_to_all | solution.py:27

commit v2 on v1

v2 whole, which is shorter than its diff:
```python
import jax
import jax.numpy as jnp
from jax import lax
from jax.experimental import pallas as pl
from jax.experimental.pallas import tpu as pltpu
from jax.sharding import Mesh, PartitionSpec as P

STEPS = 4
ROWS, COLS, MEMBERS = 32, 32, 128
PITCH = 48
LEFT = 8
HALO = STEPS
TALL = ROWS + 2 * HALO
WIDE = COLS + 2 * HALO
DEPTHS = (HALO, HALO - 1, HALO - 1)
DEEP = sum(DEPTHS)
LAT = ("y", "x")
LON = ("z", "core")

HBM = pl.BlockSpec(memory_space=pltpu.HBM)
VMEM = pl.BlockSpec(memory_space=pltpu.VMEM)
PADDED = pltpu.VMEM((TALL, PITCH, MEMBERS), jnp.float32)


def in_vmem(*shape):
    return pltpu.VMEM((*shape, MEMBERS), jnp.float32)


def flat(ref):
    return ref.reshape(ref.shape[0] * ref.shape[1], MEMBERS)


def call(kernel, outs, name, args, specs, out_specs, scratch=(), aliases=None):
    return pl.pallas_call(
        kernel,
        out_shape=outs,
        in_specs=specs,
        out_specs=out_specs,
        scratch_shapes=scratch,
        input_output_aliases=aliases or {},
        name=name,
        compiler_params=pltpu.CompilerParams(vmem_limit_bytes=16 * 2**20),
    )(*args)


def cell(row, col):
    return (row + HALO) * PITCH + LEFT + col


def columns_to_message(padded, message, at_start):
    slot = 0
    for ref, depth in zip(padded, DEPTHS):
        first = jnp.where(at_start, 0, COLS - depth)
        for k in range(depth):
            message[pl.ds(slot * ROWS, ROWS), :] = flat(ref)[pl.ds(cell(0, first + k), ROWS, stride=PITCH), :]
            slot += 1


def message_to_columns(padded, message, at_start):
    slot = 0
    for ref, depth in zip(padded, DEPTHS):
        first = jnp.where(at_start, -depth, COLS)
        for k in range(depth):
            flat(ref)[pl.ds(cell(0, first + k), ROWS, stride=PITCH), :] = message[pl.ds(slot * ROWS, ROWS), :]
            slot += 1


def rows_to_message(padded, message, at_start):
    slot = 0
    for ref, depth in zip(padded, DEPTHS):
        first = jnp.where(at_start, 0, ROWS - depth)
        for k in range(depth):
            message[slot] = ref[first + k + HALO, LEFT - HALO : LEFT - HALO + WIDE, :]
            slot += 1


def message_to_rows(padded, message, at_start):
    slot = 0
    for ref, depth in zip(padded, DEPTHS):
        first = jnp.where(at_start, -depth, ROWS)
        for k in range(depth):
            ref[first + k + HALO, LEFT - HALO : LEFT - HALO + WIDE, :] = message[slot]
            slot += 1


def load_kernel(pressure, earlier, speed, *refs):
    padded, (outer, inner), sems = refs[:3], refs[3:5], refs[5]
    copies = [
        pltpu.make_async_copy(
            source, target.at[pl.ds(HALO, ROWS), pl.ds(LEFT, COLS), :], sems.at[i]
        )
        for i, (source, target) in enumerate(zip((pressure, earlier, speed), padded))
    ]
    for copy in copies:
        copy.start()
    for copy in copies:
        copy.wait()
    first_core = lax.axis_index("core") == 0
    columns_to_message(padded, outer, first_core)
    columns_to_message(padded, inner, jnp.logical_not(first_core))


def columns_kernel(_p, _e, _s, outer, inner, *refs):
    padded, (even, odd) = refs[:3], refs[3:5]
    first_core = lax.axis_index("core") == 0
    message_to_columns(padded, outer, first_core)
    message_to_columns(padded, inner, jnp.logical_not(first_core))
    odd_x = lax.axis_index("x") % 2 == 1
    rows_to_message(padded, even, odd_x)
    rows_to_message(padded, odd, jnp.logical_not(odd_x))


def later_row(source, before, speed, row, first, width):
    cells = slice(first, first + width)
    middle = source[row, cells, :]
    spread = source[row - 1, cells, :] + source[row + 1, cells, :]
    spread += source[row, first - 1 : first - 1 + width, :]
    spread += source[row, first + 1 : first + 1 + width, :]
    spread -= 4.0 * middle
    return 2.0 * middle - before[row, cells, :] + speed[row, cells, :] * spread


def steps_kernel(_p, _e, _s, even, odd, *refs):
    padded, (end, sums, copies) = refs[:3], refs[3:6]
    odd_x = lax.axis_index("x") % 2 == 1
    message_to_rows(padded, even, odd_x)
    message_to_rows(padded, odd, jnp.logical_not(odd_x))
    now, before, speed = padded
    for step in range(STEPS - 1):
        margin = STEPS - 1 - step

        def pair(i, _, now=now, before=before, margin=margin):
            for k in range(2):
                row = HALO - margin + 2 * i + k
                before[row, LEFT - HALO : LEFT - HALO + WIDE, :] = later_row(
                    now, before, speed, row, LEFT - HALO, WIDE
                )
            return 0

        lax.fori_loop(0, (ROWS + 2 * margin) // 2, pair, 0)
        now, before = before, now

    def last(i, total):
        for k in range(2):
            row = 2 * i + k
            value = later_row(now, before, speed, row + HALO, LEFT, COLS)
            end[row] = value
            total = total + value
            sums[row] = total * (1.0 / 1024)
        return total

    total = lax.fori_loop(0, ROWS // 2, last, jnp.zeros((COLS, MEMBERS), jnp.float32))
    for k in range(copies.shape[0]):
        copies[k] = total


def middle_kernel(row, copies, before):
    here = lax.axis_index("x")
    total = jnp.zeros((COLS, MEMBERS), jnp.float32)
    for k in range(row.shape[0]):
        before[...] = jnp.where(k == here, total, before[...])
        total = total + row[k]
    for k in range(copies.shape[0]):
        copies[k] = total


def final_kernel(rows, before, sums, end, potential_out, end_out, potential, sems):
    end_copy = pltpu.make_async_copy(end, end_out, sems.at[0])
    end_copy.start()
    here = lax.axis_index("y")
    total = before[...]
    for k in range(rows.shape[0]):
        total = total + jnp.where(k < here, rows[k], 0.0)
    total = total * (1.0 / 1024)

    def add(i, _):
        for k in range(4):
            potential[4 * i + k] = sums[4 * i + k] + total
        return 0

    lax.fori_loop(0, ROWS // 4, add, 0)
    copy = pltpu.make_async_copy(potential, potential_out, sems.at[1])
    copy.start()
    copy.wait()
    end_copy.wait()


def on_device(pressure, earlier, speed_square):
    *padded, outer, inner = call(
        load_kernel,
        [PADDED] * 3 + [in_vmem(DEEP * ROWS)] * 2,
        "load",
        (pressure, earlier, speed_square),
        [HBM] * 3,
        [VMEM] * 5,
        [pltpu.SemaphoreType.DMA((3,))],
    )
    chips, ys, xs = (lax.axis_size(name) for name in ("z", "y", "x"))
    swap = lambda pairs: pairs + [(b, a) for a, b in pairs]
    outer = lax.ppermute(outer, LON, swap([(2 * z + 1, 2 * z + 2) for z in range(chips - 1)]))
    inner = lax.ppermute(inner, LON, swap([(2 * z, 2 * z + 1) for z in range(chips)]))
    same = {0: 0, 1: 1, 2: 2}
    *padded, even, odd = call(
        columns_kernel,
        [PADDED] * 3 + [in_vmem(DEEP, WIDE)] * 2,
        "columns",
        (*padded, outer, inner),
        [VMEM] * 5,
        [VMEM] * 5,
        aliases=same,
    )
    blocks = ys * xs
    even = lax.ppermute(even, LAT, swap([(i, i + 1) for i in range(0, blocks, 2)]))
    odd = lax.ppermute(odd, LAT, swap([(i, i + 1) for i in range(1, blocks - 1, 2)]))
    *_, end, sums, copies = call(
        steps_kernel,
        [PADDED] * 3 + [in_vmem(ROWS, COLS)] * 2 + [in_vmem(xs, COLS)],
        "steps",
        (*padded, even, odd),
        [VMEM] * 5,
        [VMEM] * 6,
        aliases=same,
    )
    row = lax.all_to_all(copies, "x", 0, 0, tiled=True)
    copies, before = call(
        middle_kernel,
        [in_vmem(ys, COLS), in_vmem(COLS)],
        "middle",
        (row,),
        [VMEM],
        [VMEM] * 2,
    )
    rows = lax.all_to_all(copies, "y", 0, 0, tiled=True)
    return call(
        final_kernel,
        [jax.ShapeDtypeStruct((ROWS, COLS, MEMBERS), jnp.float32)] * 2,
        "final",
        (rows, before, sums, end),
        [VMEM] * 4,
        [HBM] * 2,
        [pltpu.VMEM((ROWS, COLS, MEMBERS), jnp.float32), pltpu.SemaphoreType.DMA((2,))],
    )


def solution(mesh):
    fine = Mesh(mesh.devices.reshape(8, 4, 8, 2), ("y", "x", "z", "core"))
    spec = P(LAT, LON, None)
    return jax.shard_map(
        on_device, mesh=fine, in_specs=(spec,) * 3, out_specs=(spec,) * 2, check_vma=False
    )
```

time: 74.9 us -> 55.2 us (0.74)
  the two profiles are of different devices: /device:TPU:193 before, /device:TPU:192 now
where the time goes in v2:
time: 55.2 us; the launch traced here: 54.8 us
  blocking collectives  30.4 us (55%)
  starting transfers between devices  11.6 us (21%)
  waiting for transfers between devices  6.15 us (11%)
  local copies, waits for them, and re-layouts  3.12 us (6%)
  Pallas kernels  2.78 us (5%)
  between operations  0.71 us (1%)
    all_to_all x1, blocking collectives, on_device(): rows = lax.all_to_all(copies, 'y', 0, 0, tiled=True)  16.4 us
    all_to_all x1, blocking collectives, on_device(): row = lax.all_to_all(copies, 'x', 0, 0, tiled=True)  14 us
    ppermute x1, starting transfers between devices, on_device(): lax.ppermute(inner, LON, swap([(2 * z, 2 * z + 1) for z in range(chips)]))  5.59 us
    ppermute x1, waiting for transfers between devices, on_device(): lax.ppermute(even, LAT, swap([(i, i + 1) for i in range(0, blocks, 2)]))  5.15 us
    ppermute x1, starting transfers between devices, on_device(): lax.ppermute(even, LAT, swap([(i, i + 1) for i in range(0, blocks, 2)]))  3.4 us
    unnamed x6, local copies, waits for them, and re-layouts  3.12 us
    pallas_call x5, Pallas kernels, call(): pl.pallas_call(kernel, out_shape=outs, in_specs=specs, out_specs=out_spec...  2.78 us
    ppermute x1, starting transfers between devices, on_device(): lax.ppermute(outer, LON, swap([(2 * z + 1, 2 * z + 2) for z in range(chip...  1.92 us
  transfers between devices with their start and end apart: 4, of which 2 were waited for; matrix products, arithmetic and copies ran while one was open for 0% of the time, Pallas kernels for 0%

profile of v2, /device:TPU:192, one launch (start us, length us, event | category | flops | bytes accessed | tf_op | source)
XLA Modules:
  0.0 54.8 jit_solution(4390862306673331078)
XLA Ops:
  0.6 0.0 copy-start
  0.6 1.0 %copy-done = f32[32,32,128]{2,1,0:T(8,128)S(1)} copy-done((f32[32,32,128]{2,1,0:T(8,128)S(1)}, f32[32,32,128]{2,1,0:T(8,128)}, u32[]{:S(2)}) %copy-start) | copy-done | bytes 524312
  1.7 0.0 copy-start.1
  1.7 1.0 %copy-done.1 = f32[32,32,128]{2,1,0:T(8,128)S(1)} copy-done((f32[32,32,128]{2,1,0:T(8,128)S(1)}, f32[32,32,128]{2,1,0:T(8,128)}, u32[]{:S(2)}) %copy-start.1) | copy-done | bytes 524312
  2.7 0.0 copy-start.2
  2.7 1.0 %copy-done.2 = f32[32,32,128]{2,1,0:T(8,128)S(1)} copy-done((f32[32,32,128]{2,1,0:T(8,128)S(1)}, f32[32,32,128]{2,1,0:T(8,128)}, u32[]{:S(2)}) %copy-start.2) | copy-done | bytes 524312
  3.8 0.2 load.1
  4.0 1.9 %collective-permute-start = (f32[320,128]{1,0:T(8,128)S(1)}, f32[320,128]{1,0:T(8,128)S(1)}, u32[]{:S(2)}, u32[]{:S(2)}) collective-permute-start(f32[320,128]{1,0:T(8,128)S(1)} %get-tuple-element.20), channel_id=1, source_target_pairs={{1,2},{3,4},{5,6},{7,8},{9,10},{11,12},{13,14},{2,1},{4,3},{6,5},{... | collective-permute-start | bytes 491528 | tf_op jit(solution)/shard_map/ppermute | solution.py:200
  5.9 5.6 %collective-permute-start.1 = (f32[320,128]{1,0:T(8,128)S(1)}, f32[320,128]{1,0:T(8,128)S(1)}, u32[]{:S(2)}, u32[]{:S(2)}) collective-permute-start(f32[320,128]{1,0:T(8,128)S(1)} %get-tuple-element.21), channel_id=1, source_target_pairs={{0,1},{2,3},{4,5},{6,7},{8,9},{10,11},{12,13},{14,15},{1,0},{3,2},... | collective-permute-start | bytes 491528 | tf_op jit(solution)/shard_map/ppermute | solution.py:201
  11.5 0.0 collective-permute-done.outer
  11.6 1.0 %collective-permute-done.1.inner = f32[320,128]{1,0:T(8,128)S(1)} collective-permute-done((f32[320,128]{1,0:T(8,128)S(1)}, f32[320,128]{1,0:T(8,128)S(1)}, u32[]{:S(2)}, u32[]{:S(2)}) %collective-permute-start.1) | collective-permute-done | bytes 163872 | tf_op jit(solution)/shard_map/ppermute | solution.py:201
  12.5 0.2 columns.1
  12.7 3.4 %collective-permute-start.2 = (f32[10,40,128]{2,1,0:T(8,128)S(1)}, f32[10,40,128]{2,1,0:T(8,128)S(1)}, u32[]{:S(2)}, u32[]{:S(2)}) collective-permute-start(f32[10,40,128]{2,1,0:T(8,128)S(1)} %get-tuple-element.25), channel_id=1, source_target_pairs={{0,16},{32,48},{64,80},{96,112},{128,144},{160,176},{192,208},{224... | collective-permute-start | bytes 614408 | tf_op jit(solution)/shard_map/ppermute | solution.py:213
  16.1 0.7 %collective-permute-start.3 = (f32[10,40,128]{2,1,0:T(8,128)S(1)}, f32[10,40,128]{2,1,0:T(8,128)S(1)}, u32[]{:S(2)}, u32[]{:S(2)}) collective-permute-start(f32[10,40,128]{2,1,0:T(8,128)S(1)} %get-tuple-element.26), channel_id=1, source_target_pairs={{16,32},{48,64},{80,96},{112,128},{144,160},{176,192},{208,224},{2... | collective-permute-start | bytes 614408 | tf_op jit(solution)/shard_map/ppermute | solution.py:214
  16.8 5.2 %collective-permute-done.2.even = f32[10,40,128]{2,1,0:T(8,128)S(1)} collective-permute-done((f32[10,40,128]{2,1,0:T(8,128)S(1)}, f32[10,40,128]{2,1,0:T(8,128)S(1)}, u32[]{:S(2)}, u32[]{:S(2)}) %collective-permute-start.2) | collective-permute-done | bytes 204832 | tf_op jit(solution)/shard_map/ppermute | solution.py:213
  22.0 0.0 collective-permute-done.3.odd
  22.0 1.4 %steps.1 = (f32[40,48,128]{2,1,0:T(8,128)S(1)}, f32[40,48,128]{2,1,0:T(8,128)S(1)}, f32[40,48,128]{2,1,0:T(8,128)S(1)}, f32[32,32,128]{2,1,0:T(8,128)S(1)}, f32[...) custom-call(f32[40,48,128]{2,1,0:T(8,128)S(1)} %get-tuple-element.22, ...), custom_call_target="tpu_custom_call", output_to_operand_aliasing={{0}: (0, {}), {1}: (1, {}), {2}: (2, {})} | custom-call | tf_op jit(solution)/shard_map/steps/pallas_call | solution.py:34
  23.3 14.0 %all_to_all.10.row = f32[4,32,128]{2,1,0:T(8,128)S(1)} all-to-all(f32[4,32,128]{2,1,0:T(8,128)S(1)} %get-tuple-element.27), channel_id=1, replica_groups=mesh['y'=8,'x'=4,'z'=8,'core'=2] {'x'}, dimensions={0} | all-to-all | bytes 131072 | tf_op jit(solution)/shard_map/all_to_all | solution.py:224
  37.4 16.4 %all_to_all.11.rows = f32[8,32,128]{2,1,0:T(8,128)S(1)} all-to-all(f32[8,32,128]{2,1,0:T(8,128)S(1)} %get-tuple-element.28), channel_id=1, replica_groups=mesh['y'=8,'x'=4,'z'=8,'core'=2] {'y'}, dimensions={0} | all-to-all | bytes 262144 | tf_op jit(solution)/shard_map/all_to_all | solution.py:233
  53.8 1.0 %final.1 = (f32[32,32,128]{2,1,0:T(8,128)}, f32[32,32,128]{2,1,0:T(8,128)}) custom-call(f32[8,32,128]{2,1,0:T(8,128)S(1)} %all_to_all.11.rows, f32[32,128]{1,0:T(8,128)S(1)} %get-tuple-element.29.before, f32[32,32,128]{2,1,0:T(8,128)S(1)} %get-tuple-element.30.sums, f32[32,32,128]{2,1,0:T(8,128)S(1)} %get-tuple-element.31.end), custom_call_target="tpu_custom_call" | custom-call | tf_op jit(solution)/shard_map/final/pallas_call | solution.py:34
  (1 shorter events, 0.0 us)
Async XLA Ops:
  0.6 1.0 %copy-start = (f32[32,32,128]{2,1,0:T(8,128)S(1)}, f32[32,32,128]{2,1,0:T(8,128)}, u32[]{:S(2)}) copy-start(f32[32,32,128]{2,1,0:T(8,128)} %pressure.1) | copy-start | bytes 1572868
  1.7 1.0 %copy-start.1 = (f32[32,32,128]{2,1,0:T(8,128)S(1)}, f32[32,32,128]{2,1,0:T(8,128)}, u32[]{:S(2)}) copy-start(f32[32,32,128]{2,1,0:T(8,128)} %earlier.1) | copy-start | bytes 1572868
  2.7 1.0 %copy-start.2 = (f32[32,32,128]{2,1,0:T(8,128)S(1)}, f32[32,32,128]{2,1,0:T(8,128)}, u32[]{:S(2)}) copy-start(f32[32,32,128]{2,1,0:T(8,128)} %speed.1) | copy-start | bytes 1572868
  4.0 7.5 %collective-permute-start = (f32[320,128]{1,0:T(8,128)S(1)}, f32[320,128]{1,0:T(8,128)S(1)}, u32[]{:S(2)}, u32[]{:S(2)}) collective-permute-start(f32[320,128]{1,0:T(8,128)S(1)} %get-tuple-element.20), channel_id=1, source_target_pairs={{1,2},{3,4},{5,6},{7,8},{9,10},{11,12},{13,14},{2,1},{4,3},{6,5},{... | collective-permute-start | bytes 491528 | tf_op jit(solution)/shard_map/ppermute | solution.py:200
  5.9 6.6 %collective-permute-start.1 = (f32[320,128]{1,0:T(8,128)S(1)}, f32[320,128]{1,0:T(8,128)S(1)}, u32[]{:S(2)}, u32[]{:S(2)}) collective-permute-start(f32[320,128]{1,0:T(8,128)S(1)} %get-tuple-element.21), channel_id=1, source_target_pairs={{0,1},{2,3},{4,5},{6,7},{8,9},{10,11},{12,13},{14,15},{1,0},{3,2},... | collective-permute-start | bytes 491528 | tf_op jit(solution)/shard_map/ppermute | solution.py:201
  12.7 9.2 %collective-permute-start.2 = (f32[10,40,128]{2,1,0:T(8,128)S(1)}, f32[10,40,128]{2,1,0:T(8,128)S(1)}, u32[]{:S(2)}, u32[]{:S(2)}) collective-permute-start(f32[10,40,128]{2,1,0:T(8,128)S(1)} %get-tuple-element.25), channel_id=1, source_target_pairs={{0,16},{32,48},{64,80},{96,112},{128,144},{160,176},{192,208},{224... | collective-permute-start | bytes 614408 | tf_op jit(solution)/shard_map/ppermute | solution.py:213
  16.1 5.8 %collective-permute-start.3 = (f32[10,40,128]{2,1,0:T(8,128)S(1)}, f32[10,40,128]{2,1,0:T(8,128)S(1)}, u32[]{:S(2)}, u32[]{:S(2)}) collective-permute-start(f32[10,40,128]{2,1,0:T(8,128)S(1)} %get-tuple-element.26), channel_id=1, source_target_pairs={{16,32},{48,64},{80,96},{112,128},{144,160},{176,192},{208,224},{2... | collective-permute-start | bytes 614408 | tf_op jit(solution)/shard_map/ppermute | solution.py:214

commit v3 on v2

--- a/solution.py
+++ b/solution.py
@@ -14,6 +14,7 @@
 WIDE = COLS + 2 * HALO
 DEPTHS = (HALO, HALO - 1, HALO - 1)
 DEEP = sum(DEPTHS)
+PIECES = 4
 LAT = ("y", "x")
 LON = ("z", "core")
 
@@ -85,11 +86,15 @@
 
 def load_kernel(pressure, earlier, speed, *refs):
     padded, (outer, inner), sems = refs[:3], refs[3:5], refs[5]
+    piece = ROWS // PIECES
     copies = [
         pltpu.make_async_copy(
-            source, target.at[pl.ds(HALO, ROWS), pl.ds(LEFT, COLS), :], sems.at[i]
+            source.at[pl.ds(k * piece, piece)],
+            target.at[pl.ds(HALO + k * piece, piece), pl.ds(LEFT, COLS), :],
+            sems.at[i, k],
         )
         for i, (source, target) in enumerate(zip((pressure, earlier, speed), padded))
+        for k in range(PIECES)
     ]
     for copy in copies:
         copy.start()
@@ -120,7 +125,7 @@
     return 2.0 * middle - before[row, cells, :] + speed[row, cells, :] * spread
 
 
-def steps_kernel(_p, _e, _s, even, odd, *refs):
+def steps_kernel(_p, _e, _s, odd, even, *refs):
     padded, (end, sums, copies) = refs[:3], refs[3:6]
     odd_x = lax.axis_index("x") % 2 == 1
     message_to_rows(padded, even, odd_x)
@@ -190,10 +195,10 @@
         load_kernel,
         [PADDED] * 3 + [in_vmem(DEEP * ROWS)] * 2,
         "load",
-        (pressure, earlier, speed_square),
+        [pltpu.with_memory_space_constraint(a, pltpu.HBM) for a in (pressure, earlier, speed_square)],
         [HBM] * 3,
         [VMEM] * 5,
-        [pltpu.SemaphoreType.DMA((3,))],
+        [pltpu.SemaphoreType.DMA((3, PIECES))],
     )
     chips, ys, xs = (lax.axis_size(name) for name in ("z", "y", "x"))
     swap = lambda pairs: pairs + [(b, a) for a, b in pairs]
@@ -210,13 +215,13 @@
         aliases=same,
     )
     blocks = ys * xs
+    odd = lax.ppermute(odd, LAT, swap([(i, i + 1) for i in range(1, blocks - 1, 2)]))
     even = lax.ppermute(even, LAT, swap([(i, i + 1) for i in range(0, blocks, 2)]))
-    odd = lax.ppermute(odd, LAT, swap([(i, i + 1) for i in range(1, blocks - 1, 2)]))
     *_, end, sums, copies = call(
         steps_kernel,
         [PADDED] * 3 + [in_vmem(ROWS, COLS)] * 2 + [in_vmem(xs, COLS)],
         "steps",
-        (*padded, even, odd),
+        (*padded, odd, even),
         [VMEM] * 5,
         [VMEM] * 6,
         aliases=same,

time: 55.2 us -> 51.3 us (0.929)
  blocking collectives: 30.4 us -> 25.5 us
  local copies, waits for them, and re-layouts: 3.12 us -> 0 us
  starting transfers between devices: 11.6 us -> 14.3 us
  Pallas kernels: 2.78 us -> 4.18 us
    all_to_all x1, blocking collectives: 14 us -> 9.7 us  [on_device(): row = lax.all_to_all(copies, 'x', 0, 0, tiled=True)]
    unnamed x6 -> x0, local copies, waits for them, and re-layouts: 3.12 us -> none
    ppermute x1, starting transfers between devices: 3.4 us -> 6.13 us  [on_device(): lax.ppermute(even, LAT, swap([(i, i + 1) for i in range(0, blocks, 2)]))]
    pallas_call x5, Pallas kernels: 2.78 us -> 4.18 us  [call(): pl.pallas_call(kernel, out_shape=outs, in_specs=specs, out_specs=out_spec...]
    all_to_all x1, blocking collectives: 16.4 us -> 15.8 us  [on_device(): rows = lax.all_to_all(copies, 'y', 0, 0, tiled=True)]
where the time goes in v3:
time: 51.3 us; the launch traced here: 51 us
  blocking collectives  25.5 us (50%)
  starting transfers between devices  14.3 us (28%)
  waiting for transfers between devices  6.3 us (12%)
  Pallas kernels  4.18 us (8%)
  between operations  0.71 us (1%)
    all_to_all x1, blocking collectives, on_device(): rows = lax.all_to_all(copies, 'y', 0, 0, tiled=True)  15.8 us
    all_to_all x1, blocking collectives, on_device(): row = lax.all_to_all(copies, 'x', 0, 0, tiled=True)  9.7 us
    ppermute x1, starting transfers between devices, on_device(): lax.ppermute(even, LAT, swap([(i, i + 1) for i in range(0, blocks, 2)]))  6.13 us
    ppermute x1, starting transfers between devices, on_device(): lax.ppermute(inner, LON, swap([(2 * z, 2 * z + 1) for z in range(chips)]))  5.59 us
    ppermute x1, waiting for transfers between devices, on_device(): lax.ppermute(even, LAT, swap([(i, i + 1) for i in range(0, blocks, 2)]))  5.3 us
    pallas_call x5, Pallas kernels, call(): pl.pallas_call(kernel, out_shape=outs, in_specs=specs, out_specs=out_spec...  4.18 us
    ppermute x1, starting transfers between devices, on_device(): lax.ppermute(outer, LON, swap([(2 * z + 1, 2 * z + 2) for z in range(chip...  1.92 us
  transfers between devices with their start and end apart: 4, of which 2 were waited for; matrix products, arithmetic and copies ran while one was open for 0% of the time, Pallas kernels for 0%

profile of v3, /device:TPU:192, one launch (start us, length us, event | category | flops | bytes accessed | tf_op | source)
XLA Modules:
  0.0 51.0 jit_solution(17537361263627786093)
XLA Ops:
  0.6 1.6 %load.1 = (f32[40,48,128]{2,1,0:T(8,128)S(1)}, f32[40,48,128]{2,1,0:T(8,128)S(1)}, f32[40,48,128]{2,1,0:T(8,128)S(1)}, f32[320,128]{1,0:T(8,128)S(1)}, f32[320,128]{1,0:T(8,128)S(1)}) custom-call(f32[32,32,128]{2,1,0:T(8,128)} %pressure.1, f32[32,32,128]{2,1,0:T(8,128)} %earlier.1, f32[32,32,128]{2,1,0:T(8,128)} %speed.1), custom_call_target="tpu_custom_call" | custom-call | tf_op jit(solution)/shard_map/load/pallas_call | solution.py:35
  2.3 1.9 %collective-permute-start = (f32[320,128]{1,0:T(8,128)S(1)}, f32[320,128]{1,0:T(8,128)S(1)}, u32[]{:S(2)}, u32[]{:S(2)}) collective-permute-start(f32[320,128]{1,0:T(8,128)S(1)} %get-tuple-element.20), channel_id=1, source_target_pairs={{1,2},{3,4},{5,6},{7,8},{9,10},{11,12},{13,14},{2,1},{4,3},{6,5},{... | collective-permute-start | bytes 491528 | tf_op jit(solution)/shard_map/ppermute | solution.py:205
  4.2 5.6 %collective-permute-start.1 = (f32[320,128]{1,0:T(8,128)S(1)}, f32[320,128]{1,0:T(8,128)S(1)}, u32[]{:S(2)}, u32[]{:S(2)}) collective-permute-start(f32[320,128]{1,0:T(8,128)S(1)} %get-tuple-element.21), channel_id=1, source_target_pairs={{0,1},{2,3},{4,5},{6,7},{8,9},{10,11},{12,13},{14,15},{1,0},{3,2},... | collective-permute-start | bytes 491528 | tf_op jit(solution)/shard_map/ppermute | solution.py:206
  9.8 0.0 collective-permute-done.outer
  9.8 1.0 %collective-permute-done.1.inner = f32[320,128]{1,0:T(8,128)S(1)} collective-permute-done((f32[320,128]{1,0:T(8,128)S(1)}, f32[320,128]{1,0:T(8,128)S(1)}, u32[]{:S(2)}, u32[]{:S(2)}) %collective-permute-start.1) | collective-permute-done | bytes 163872 | tf_op jit(solution)/shard_map/ppermute | solution.py:206
  10.8 0.2 columns.1
  11.0 0.7 %collective-permute-start.2 = (f32[10,40,128]{2,1,0:T(8,128)S(1)}, f32[10,40,128]{2,1,0:T(8,128)S(1)}, u32[]{:S(2)}, u32[]{:S(2)}) collective-permute-start(f32[10,40,128]{2,1,0:T(8,128)S(1)} %get-tuple-element.25), channel_id=1, source_target_pairs={{16,32},{48,64},{80,96},{112,128},{144,160},{176,192},{208,224},{2... | collective-permute-start | bytes 614408 | tf_op jit(solution)/shard_map/ppermute | solution.py:218
  11.7 6.1 %collective-permute-start.3 = (f32[10,40,128]{2,1,0:T(8,128)S(1)}, f32[10,40,128]{2,1,0:T(8,128)S(1)}, u32[]{:S(2)}, u32[]{:S(2)}) collective-permute-start(f32[10,40,128]{2,1,0:T(8,128)S(1)} %get-tuple-element.26), channel_id=1, source_target_pairs={{0,16},{32,48},{64,80},{96,112},{128,144},{160,176},{192,208},{224... | collective-permute-start | bytes 614408 | tf_op jit(solution)/shard_map/ppermute | solution.py:219
  17.8 0.0 collective-permute-done.2.odd
  17.8 5.3 %collective-permute-done.3.even = f32[10,40,128]{2,1,0:T(8,128)S(1)} collective-permute-done((f32[10,40,128]{2,1,0:T(8,128)S(1)}, f32[10,40,128]{2,1,0:T(8,128)S(1)}, u32[]{:S(2)}, u32[]{:S(2)}) %collective-permute-start.3) | collective-permute-done | bytes 204832 | tf_op jit(solution)/shard_map/ppermute | solution.py:219
  23.1 1.4 %steps.1 = (f32[40,48,128]{2,1,0:T(8,128)S(1)}, f32[40,48,128]{2,1,0:T(8,128)S(1)}, f32[40,48,128]{2,1,0:T(8,128)S(1)}, f32[32,32,128]{2,1,0:T(8,128)S(1)}, f32[...) custom-call(f32[40,48,128]{2,1,0:T(8,128)S(1)} %get-tuple-element.22, ...), custom_call_target="tpu_custom_call", output_to_operand_aliasing={{0}: (0, {}), {1}: (1, {}), {2}: (2, {})} | custom-call | tf_op jit(solution)/shard_map/steps/pallas_call | solution.py:35
  24.5 9.7 %all_to_all.10.row = f32[4,32,128]{2,1,0:T(8,128)S(1)} all-to-all(f32[4,32,128]{2,1,0:T(8,128)S(1)} %get-tuple-element.27), channel_id=1, replica_groups=mesh['y'=8,'x'=4,'z'=8,'core'=2] {'x'}, dimensions={0} | all-to-all | bytes 131072 | tf_op jit(solution)/shard_map/all_to_all | solution.py:229
  34.2 15.8 %all_to_all.11.rows = f32[8,32,128]{2,1,0:T(8,128)S(1)} all-to-all(f32[8,32,128]{2,1,0:T(8,128)S(1)} %get-tuple-element.28), channel_id=1, replica_groups=mesh['y'=8,'x'=4,'z'=8,'core'=2] {'y'}, dimensions={0} | all-to-all | bytes 262144 | tf_op jit(solution)/shard_map/all_to_all | solution.py:238
  50.0 1.0 %final.1 = (f32[32,32,128]{2,1,0:T(8,128)}, f32[32,32,128]{2,1,0:T(8,128)}) custom-call(f32[8,32,128]{2,1,0:T(8,128)S(1)} %all_to_all.11.rows, f32[32,128]{1,0:T(8,128)S(1)} %get-tuple-element.29.before, f32[32,32,128]{2,1,0:T(8,128)S(1)} %get-tuple-element.30.sums, f32[32,32,128]{2,1,0:T(8,128)S(1)} %get-tuple-element.31.end), custom_call_target="tpu_custom_call" | custom-call | tf_op jit(solution)/shard_map/final/pallas_call | solution.py:35
  (1 shorter events, 0.0 us)
Async XLA Ops:
  2.3 7.5 %collective-permute-start = (f32[320,128]{1,0:T(8,128)S(1)}, f32[320,128]{1,0:T(8,128)S(1)}, u32[]{:S(2)}, u32[]{:S(2)}) collective-permute-start(f32[320,128]{1,0:T(8,128)S(1)} %get-tuple-element.20), channel_id=1, source_target_pairs={{1,2},{3,4},{5,6},{7,8},{9,10},{11,12},{13,14},{2,1},{4,3},{6,5},{... | collective-permute-start | bytes 491528 | tf_op jit(solution)/shard_map/ppermute | solution.py:205
  4.2 6.6 %collective-permute-start.1 = (f32[320,128]{1,0:T(8,128)S(1)}, f32[320,128]{1,0:T(8,128)S(1)}, u32[]{:S(2)}, u32[]{:S(2)}) collective-permute-start(f32[320,128]{1,0:T(8,128)S(1)} %get-tuple-element.21), channel_id=1, source_target_pairs={{0,1},{2,3},{4,5},{6,7},{8,9},{10,11},{12,13},{14,15},{1,0},{3,2},... | collective-permute-start | bytes 491528 | tf_op jit(solution)/shard_map/ppermute | solution.py:206
  11.0 6.8 %collective-permute-start.2 = (f32[10,40,128]{2,1,0:T(8,128)S(1)}, f32[10,40,128]{2,1,0:T(8,128)S(1)}, u32[]{:S(2)}, u32[]{:S(2)}) collective-permute-start(f32[10,40,128]{2,1,0:T(8,128)S(1)} %get-tuple-element.25), channel_id=1, source_target_pairs={{16,32},{48,64},{80,96},{112,128},{144,160},{176,192},{208,224},{2... | collective-permute-start | bytes 614408 | tf_op jit(solution)/shard_map/ppermute | solution.py:218
  11.7 11.4 %collective-permute-start.3 = (f32[10,40,128]{2,1,0:T(8,128)S(1)}, f32[10,40,128]{2,1,0:T(8,128)S(1)}, u32[]{:S(2)}, u32[]{:S(2)}) collective-permute-start(f32[10,40,128]{2,1,0:T(8,128)S(1)} %get-tuple-element.26), channel_id=1, source_target_pairs={{0,16},{32,48},{64,80},{96,112},{128,144},{160,176},{192,208},{224... | collective-permute-start | bytes 614408 | tf_op jit(solution)/shard_map/ppermute | solution.py:219

commit v4 on v3

--- a/solution.py
+++ b/solution.py
@@ -7,7 +7,7 @@
 
 STEPS = 4
 ROWS, COLS, MEMBERS = 32, 32, 128
-PITCH = 48
+PITCH = 56
 LEFT = 8
 HALO = STEPS
 TALL = ROWS + 2 * HALO
@@ -15,11 +15,15 @@
 DEPTHS = (HALO, HALO - 1, HALO - 1)
 DEEP = sum(DEPTHS)
 PIECES = 4
+FINAL_PIECES = 4
+INSIDE = ROWS - 2 * STEPS
+SCALE = 1.0 / 1024
 LAT = ("y", "x")
 LON = ("z", "core")
 
 HBM = pl.BlockSpec(memory_space=pltpu.HBM)
 VMEM = pl.BlockSpec(memory_space=pltpu.VMEM)
+WHOLE = pltpu.HBM((ROWS, COLS, MEMBERS), jnp.float32)
 PADDED = pltpu.VMEM((TALL, PITCH, MEMBERS), jnp.float32)
 
 
@@ -31,7 +35,7 @@
     return ref.reshape(ref.shape[0] * ref.shape[1], MEMBERS)
 
 
-def call(kernel, outs, name, args, specs, out_specs, scratch=(), aliases=None):
+def call(kernel, outs, name, args, specs, out_specs, scratch=(), aliases=None, flops=10**5):
     return pl.pallas_call(
         kernel,
         out_shape=outs,
@@ -40,6 +44,7 @@
         scratch_shapes=scratch,
         input_output_aliases=aliases or {},
         name=name,
+        cost_estimate=pl.CostEstimate(flops=flops, bytes_accessed=0, transcendentals=0),
         compiler_params=pltpu.CompilerParams(vmem_limit_bytes=16 * 2**20),
     )(*args)
 
@@ -67,21 +72,23 @@
 
 
 def rows_to_message(padded, message, at_start):
-    slot = 0
-    for ref, depth in zip(padded, DEPTHS):
-        first = jnp.where(at_start, 0, ROWS - depth)
-        for k in range(depth):
-            message[slot] = ref[first + k + HALO, LEFT - HALO : LEFT - HALO + WIDE, :]
-            slot += 1
+    now, before, speed = padded
+    first, second, third = (HALO + jnp.where(at_start, k, ROWS - 1 - k) for k in range(3))
+    cells = slice(LEFT - HALO, LEFT - HALO + WIDE)
+    beyond = speed[second, cells, :] * later_row(now, before, speed, third, LEFT - HALO, WIDE)
+    message[0] = now[first, cells, :]
+    message[1] = now[second, cells, :] - beyond
+    message[2] = before[first, cells, :] - speed[first, cells, :] * beyond
+    message[3] = later_row(now, before, speed, second, LEFT - HALO, WIDE)
+    message[4] = speed[first, cells, :]
+    message[5] = speed[second, cells, :]
 
 
 def message_to_rows(padded, message, at_start):
-    slot = 0
-    for ref, depth in zip(padded, DEPTHS):
-        first = jnp.where(at_start, -depth, ROWS)
-        for k in range(depth):
-            ref[first + k + HALO, LEFT - HALO : LEFT - HALO + WIDE, :] = message[slot]
-            slot += 1
+    for k in range(2):
+        row = HALO + jnp.where(at_start, -1 - k, ROWS + k)
+        for slot, ref in enumerate(padded):
+            ref[row, LEFT - HALO : LEFT - HALO + WIDE, :] = message[2 * slot + k]
 
 
 def load_kernel(pressure, earlier, speed, *refs):
@@ -106,13 +113,15 @@
 
 
 def columns_kernel(_p, _e, _s, outer, inner, *refs):
-    padded, (even, odd) = refs[:3], refs[3:5]
+    padded, (odd, even) = refs[:3], refs[3:5]
     first_core = lax.axis_index("core") == 0
     message_to_columns(padded, outer, first_core)
     message_to_columns(padded, inner, jnp.logical_not(first_core))
     odd_x = lax.axis_index("x") % 2 == 1
+    rows_to_message(padded, odd, jnp.logical_not(odd_x))
     rows_to_message(padded, even, odd_x)
-    rows_to_message(padded, odd, jnp.logical_not(odd_x))
+    for row in (HALO - 3, HALO + ROWS + 2):
+        padded[1][row] = jnp.zeros((PITCH, MEMBERS), jnp.float32)
 
 
 def later_row(source, before, speed, row, first, width):
@@ -125,36 +134,64 @@
     return 2.0 * middle - before[row, cells, :] + speed[row, cells, :] * spread
 
 
-def steps_kernel(_p, _e, _s, odd, even, *refs):
-    padded, (end, sums, copies) = refs[:3], refs[3:6]
-    odd_x = lax.axis_index("x") % 2 == 1
-    message_to_rows(padded, even, odd_x)
-    message_to_rows(padded, odd, jnp.logical_not(odd_x))
+def set_later_row(source, before, speed, row):
+    cells = slice(LEFT - HALO, LEFT - HALO + WIDE)
+    before[row, cells, :] = later_row(source, before, speed, row, LEFT - HALO, WIDE)
+
+
+def inner_kernel(_p, _e, _s, *refs):
+    padded, (end_out, sums, total_out, end, sem) = refs[:3], refs[3:]
     now, before, speed = padded
-    for step in range(STEPS - 1):
-        margin = STEPS - 1 - step
-
-        def pair(i, _, now=now, before=before, margin=margin):
+    for step in range(1, STEPS):
+
+        def pair(i, _, now=now, before=before, step=step):
             for k in range(2):
-                row = HALO - margin + 2 * i + k
-                before[row, LEFT - HALO : LEFT - HALO + WIDE, :] = later_row(
-                    now, before, speed, row, LEFT - HALO, WIDE
-                )
+                set_later_row(now, before, speed, HALO + step + 2 * i + k)
             return 0
 
-        lax.fori_loop(0, (ROWS + 2 * margin) // 2, pair, 0)
+        lax.fori_loop(0, (ROWS - 2 * step) // 2, pair, 0)
         now, before = before, now
 
     def last(i, total):
         for k in range(2):
             row = 2 * i + k
-            value = later_row(now, before, speed, row + HALO, LEFT, COLS)
+            value = later_row(now, before, speed, row + HALO + STEPS, LEFT, COLS)
             end[row] = value
             total = total + value
-            sums[row] = total * (1.0 / 1024)
+            sums[row] = total * SCALE
         return total
 
-    total = lax.fori_loop(0, ROWS // 2, last, jnp.zeros((COLS, MEMBERS), jnp.float32))
+    total_out[...] = lax.fori_loop(0, INSIDE // 2, last, jnp.zeros((COLS, MEMBERS), jnp.float32))
+    copy = pltpu.make_async_copy(end, end_out.at[pl.ds(STEPS, INSIDE)], sem)
+    copy.start()
+    copy.wait()
+
+
+def edges_kernel(_p, _e, _s, odd, even, inside, *refs):
+    padded, (end, sums, offsets, copies) = refs[:3], refs[3:]
+    odd_x = lax.axis_index("x") % 2 == 1
+    message_to_rows(padded, odd, jnp.logical_not(odd_x))
+    message_to_rows(padded, even, odd_x)
+    now, before, speed = padded
+    for first, count in ((-1, 2), (-2, 4), (-1, 4)):
+        for k in range(count):
+            set_later_row(now, before, speed, HALO + first + k)
+            set_later_row(now, before, speed, HALO + ROWS - 1 - first - k)
+        now, before = before, now
+    total = jnp.zeros((COLS, MEMBERS), jnp.float32)
+    for side in range(2):
+        here = jnp.zeros((COLS, MEMBERS), jnp.float32)
+        for k in range(STEPS):
+            row = side * (ROWS - STEPS) + k
+            value = later_row(now, before, speed, row + HALO, LEFT, COLS)
+            end[side * STEPS + k] = value
+            here = here + value
+            sums[side * STEPS + k] = here * SCALE
+        total = total + here
+        if side == 0:
+            offsets[0] = total * SCALE
+            total = total + inside[...]
+            offsets[1] = total * SCALE
     for k in range(copies.shape[0]):
         copies[k] = total
 
@@ -169,25 +206,36 @@
         copies[k] = total
 
 
-def final_kernel(rows, before, sums, end, potential_out, end_out, potential, sems):
-    end_copy = pltpu.make_async_copy(end, end_out, sems.at[0])
-    end_copy.start()
+def final_kernel(rows, before, inner_sums, edge_sums, offsets, edges, _end, potential_out, end_out, potential, sems):
+    copies = [
+        pltpu.make_async_copy(edges.at[pl.ds(0, STEPS)], end_out.at[pl.ds(0, STEPS)], sems.at[0]),
+        pltpu.make_async_copy(
+            edges.at[pl.ds(STEPS, STEPS)], end_out.at[pl.ds(ROWS - STEPS, STEPS)], sems.at[1]
+        ),
+    ]
+    for copy in copies:
+        copy.start()
     here = lax.axis_index("y")
     total = before[...]
     for k in range(rows.shape[0]):
         total = total + jnp.where(k < here, rows[k], 0.0)
-    total = total * (1.0 / 1024)
-
-    def add(i, _):
-        for k in range(4):
-            potential[4 * i + k] = sums[4 * i + k] + total
-        return 0
-
-    lax.fori_loop(0, ROWS // 4, add, 0)
-    copy = pltpu.make_async_copy(potential, potential_out, sems.at[1])
-    copy.start()
-    copy.wait()
-    end_copy.wait()
+    total = total * SCALE
+    upper = total + offsets[1]
+    for k in range(STEPS):
+        potential[k] = edge_sums[k] + total
+        potential[ROWS - STEPS + k] = edge_sums[STEPS + k] + upper
+    inner = total + offsets[0]
+    piece = ROWS // FINAL_PIECES
+    for part in range(FINAL_PIECES):
+        for row in range(part * piece, (part + 1) * piece):
+            if STEPS <= row < ROWS - STEPS:
+                potential[row] = inner_sums[row - STEPS] + inner
+        place = pl.ds(part * piece, piece)
+        copy = pltpu.make_async_copy(potential.at[place], potential_out.at[place], sems.at[2 + part])
+        copy.start()
+        copies.append(copy)
+    for copy in copies:
+        copy.wait()
 
 
 def on_device(pressure, earlier, speed_square):
@@ -205,9 +253,9 @@
     outer = lax.ppermute(outer, LON, swap([(2 * z + 1, 2 * z + 2) for z in range(chips - 1)]))
     inner = lax.ppermute(inner, LON, swap([(2 * z, 2 * z + 1) for z in range(chips)]))
     same = {0: 0, 1: 1, 2: 2}
-    *padded, even, odd = call(
+    *padded, odd, even = call(
         columns_kernel,
-        [PADDED] * 3 + [in_vmem(DEEP, WIDE)] * 2,
+        [PADDED] * 3 + [in_vmem(6, WIDE)] * 2,
         "columns",
         (*padded, outer, inner),
         [VMEM] * 5,
@@ -217,13 +265,24 @@
     blocks = ys * xs
     odd = lax.ppermute(odd, LAT, swap([(i, i + 1) for i in range(1, blocks - 1, 2)]))
     even = lax.ppermute(even, LAT, swap([(i, i + 1) for i in range(0, blocks, 2)]))
-    *_, end, sums, copies = call(
-        steps_kernel,
-        [PADDED] * 3 + [in_vmem(ROWS, COLS)] * 2 + [in_vmem(xs, COLS)],
-        "steps",
-        (*padded, odd, even),
-        [VMEM] * 5,
+    *padded, end, inner_sums, inside = call(
+        inner_kernel,
+        [PADDED] * 3 + [WHOLE, in_vmem(INSIDE, COLS), in_vmem(COLS)],
+        "inner",
+        padded,
+        [VMEM] * 3,
+        [VMEM] * 3 + [HBM] + [VMEM] * 2,
+        [in_vmem(INSIDE, COLS), pltpu.SemaphoreType.DMA],
+        aliases=same,
+        flops=10**8,
+    )
+    *_, edges, edge_sums, offsets, copies = call(
+        edges_kernel,
+        [PADDED] * 3 + [in_vmem(2 * STEPS, COLS)] * 2 + [in_vmem(2, COLS), in_vmem(xs, COLS)],
+        "edges",
+        (*padded, odd, even, inside),
         [VMEM] * 6,
+        [VMEM] * 7,
         aliases=same,
     )
     row = lax.all_to_all(copies, "x", 0, 0, tiled=True)
@@ -238,12 +297,13 @@
     rows = lax.all_to_all(copies, "y", 0, 0, tiled=True)
     return call(
         final_kernel,
-        [jax.ShapeDtypeStruct((ROWS, COLS, MEMBERS), jnp.float32)] * 2,
+        [WHOLE] * 2,
         "final",
-        (rows, before, sums, end),
-        [VMEM] * 4,
+        (rows, before, inner_sums, edge_sums, offsets, edges, end),
+        [VMEM] * 6 + [HBM],
         [HBM] * 2,
-        [pltpu.VMEM((ROWS, COLS, MEMBERS), jnp.float32), pltpu.SemaphoreType.DMA((2,))],
+        [in_vmem(ROWS, COLS), pltpu.SemaphoreType.DMA((2 + FINAL_PIECES,))],
+        aliases={6: 1},
     )
 
 

time: 51.3 us -> 48.2 us (0.940)
  waiting for transfers between devices: 6.3 us -> 2.75 us
    ppermute x1, waiting for transfers between devices: 5.3 us -> 1.75 us  [on_device(): lax.ppermute(even, LAT, swap([(i, i + 1) for i in range(0, blocks, 2)]))]
    pallas_call x5 -> x6, Pallas kernels: 4.18 us -> 4.61 us  [call(): pl.pallas_call(kernel, out_shape=outs, in_specs=specs, out_specs=out_spec...]
  transfers between devices with their start and end apart: 4 -> 4, of which waited for: 2 -> 2; matrix products, arithmetic and copies ran while one was open for 0% -> 0% of each run, Pallas kernels for 0% -> 4%
where the time goes in v4:
time: 48.2 us; the launch traced here: 47.9 us
  blocking collectives  25.5 us (53%)
  starting transfers between devices  14.3 us (30%)
  Pallas kernels  4.61 us (10%)
  waiting for transfers between devices  2.75 us (6%)
  between operations  0.71 us (1%)
    all_to_all x1, blocking collectives, on_device(): rows = lax.all_to_all(copies, 'y', 0, 0, tiled=True)  15.8 us
    all_to_all x1, blocking collectives, on_device(): row = lax.all_to_all(copies, 'x', 0, 0, tiled=True)  9.7 us
    ppermute x1, starting transfers between devices, on_device(): lax.ppermute(even, LAT, swap([(i, i + 1) for i in range(0, blocks, 2)]))  6.13 us
    ppermute x1, starting transfers between devices, on_device(): lax.ppermute(inner, LON, swap([(2 * z, 2 * z + 1) for z in range(chips)]))  5.59 us
    pallas_call x6, Pallas kernels, call(): pl.pallas_call(kernel, out_shape=outs, in_specs=specs, out_specs=out_spec...  4.61 us
    ppermute x1, starting transfers between devices, on_device(): lax.ppermute(outer, LON, swap([(2 * z + 1, 2 * z + 2) for z in range(chip...  1.92 us
    ppermute x1, waiting for transfers between devices, on_device(): lax.ppermute(even, LAT, swap([(i, i + 1) for i in range(0, blocks, 2)]))  1.75 us
    ppermute x1, waiting for transfers between devices, on_device(): lax.ppermute(inner, LON, swap([(2 * z, 2 * z + 1) for z in range(chips)]))  1 us
  transfers between devices with their start and end apart: 4, of which 2 were waited for; matrix products, arithmetic and copies ran while one was open for 0% of the time, Pallas kernels for 4%

profile of v4, /device:TPU:192, one launch (start us, length us, event | category | flops | bytes accessed | tf_op | source)
XLA Modules:
  0.0 47.9 jit_solution(5542243934227593765)
XLA Ops:
  0.6 1.6 %load.1 = (f32[40,56,128]{2,1,0:T(8,128)S(1)}, f32[40,56,128]{2,1,0:T(8,128)S(1)}, f32[40,56,128]{2,1,0:T(8,128)S(1)}, f32[320,128]{1,0:T(8,128)S(1)}, f32[320,128]{1,0:T(8,128)S(1)}) custom-call(f32[32,32,128]{2,1,0:T(8,128)} %pressure.1, f32[32,32,128]{2,1,0:T(8,128)} %earlier.1, f32[32,32,128]{2,1,0:T(8,128)} %speed.1), custom_call_target="tpu_custom_call" | custom-call | flops 100000 | tf_op jit(solution)/shard_map/load/pallas_call | solution.py:39
  2.2 1.9 %collective-permute-start = (f32[320,128]{1,0:T(8,128)S(1)}, f32[320,128]{1,0:T(8,128)S(1)}, u32[]{:S(2)}, u32[]{:S(2)}) collective-permute-start(f32[320,128]{1,0:T(8,128)S(1)} %get-tuple-element.27), channel_id=1, source_target_pairs={{1,2},{3,4},{5,6},{7,8},{9,10},{11,12},{13,14},{2,1},{4,3},{6,5},{... | collective-permute-start | bytes 491528 | tf_op jit(solution)/shard_map/ppermute | solution.py:253
  4.2 5.6 %collective-permute-start.1 = (f32[320,128]{1,0:T(8,128)S(1)}, f32[320,128]{1,0:T(8,128)S(1)}, u32[]{:S(2)}, u32[]{:S(2)}) collective-permute-start(f32[320,128]{1,0:T(8,128)S(1)} %get-tuple-element.28), channel_id=1, source_target_pairs={{0,1},{2,3},{4,5},{6,7},{8,9},{10,11},{12,13},{14,15},{1,0},{3,2},... | collective-permute-start | bytes 491528 | tf_op jit(solution)/shard_map/ppermute | solution.py:254
  9.8 0.0 collective-permute-done.outer
  9.8 1.0 %collective-permute-done.1.inner = f32[320,128]{1,0:T(8,128)S(1)} collective-permute-done((f32[320,128]{1,0:T(8,128)S(1)}, f32[320,128]{1,0:T(8,128)S(1)}, u32[]{:S(2)}, u32[]{:S(2)}) %collective-permute-start.1) | collective-permute-done | bytes 163872 | tf_op jit(solution)/shard_map/ppermute | solution.py:254
  10.8 0.1 columns.1
  10.9 0.7 %collective-permute-start.2 = (f32[6,40,128]{2,1,0:T(8,128)S(1)}, f32[6,40,128]{2,1,0:T(8,128)S(1)}, u32[]{:S(2)}, u32[]{:S(2)}) collective-permute-start(f32[6,40,128]{2,1,0:T(8,128)S(1)} %get-tuple-element.35), channel_id=1, source_target_pairs={{16,32},{48,64},{80,96},{112,128},{144,160},{176,192},{208,224},{2... | collective-permute-start | bytes 368648 | tf_op jit(solution)/shard_map/ppermute | solution.py:266
  11.6 6.1 %collective-permute-start.3 = (f32[6,40,128]{2,1,0:T(8,128)S(1)}, f32[6,40,128]{2,1,0:T(8,128)S(1)}, u32[]{:S(2)}, u32[]{:S(2)}) collective-permute-start(f32[6,40,128]{2,1,0:T(8,128)S(1)} %get-tuple-element.36), channel_id=1, source_target_pairs={{0,16},{32,48},{64,80},{96,112},{128,144},{160,176},{192,208},{224... | collective-permute-start | bytes 368648 | tf_op jit(solution)/shard_map/ppermute | solution.py:267
  17.7 1.8 %inner.1 = (f32[40,56,128]{2,1,0:T(8,128)S(1)}, f32[40,56,128]{2,1,0:T(8,128)S(1)}, f32[40,56,128]{2,1,0:T(8,128)S(1)}, f32[32,32,128]{2,1,0:T(8,128)}, f32[24,3...) custom-call(f32[40,56,128]{2,1,0:T(8,128)S(1)} %get-tuple-element.29._p, ...), custom_call_target="tpu_custom_call", output_to_operand_aliasing={{0}: (0, {}), {1}: (1, {}), {2}: (2, {})} | custom-call | flops 100000000 | tf_op jit(solution)/shard_map/inner/pallas_call | solution.py:39
  19.5 0.0 collective-permute-done.2.odd
  19.5 1.8 %collective-permute-done.3.even = f32[6,40,128]{2,1,0:T(8,128)S(1)} collective-permute-done((f32[6,40,128]{2,1,0:T(8,128)S(1)}, f32[6,40,128]{2,1,0:T(8,128)S(1)}, u32[]{:S(2)}, u32[]{:S(2)}) %collective-permute-start.3) | collective-permute-done | bytes 122912 | tf_op jit(solution)/shard_map/ppermute | solution.py:267
  21.3 0.2 edges.1
  21.5 9.7 %all_to_all.10.row = f32[4,32,128]{2,1,0:T(8,128)S(1)} all-to-all(f32[4,32,128]{2,1,0:T(8,128)S(1)} %get-tuple-element.38), channel_id=1, replica_groups=mesh['y'=8,'x'=4,'z'=8,'core'=2] {'x'}, dimensions={0} | all-to-all | bytes 131072 | tf_op jit(solution)/shard_map/all_to_all | solution.py:288
  31.2 15.8 %all_to_all.11.rows = f32[8,32,128]{2,1,0:T(8,128)S(1)} all-to-all(f32[8,32,128]{2,1,0:T(8,128)S(1)} %get-tuple-element.39), channel_id=1, replica_groups=mesh['y'=8,'x'=4,'z'=8,'core'=2] {'y'}, dimensions={0} | all-to-all | bytes 262144 | tf_op jit(solution)/shard_map/all_to_all | solution.py:297
  47.0 0.9 %final.1 = (f32[32,32,128]{2,1,0:T(8,128)}, f32[32,32,128]{2,1,0:T(8,128)}) custom-call(f32[8,32,128]{2,1,0:T(8,128)S(1)} %all_to_all.11.rows, f32[32,128]{1,0:T(8,128)S(1)} %get-tuple-element.40.before, f32[24,32,128]{2,1,0:T(8,128)S(1)} %get-tuple-element.41.inner_sums, ...), custom_call_target="tpu_custom_call", output_to_operand_aliasing={{1}: (6, {})} | custom-call | flops 100000 | tf_op jit(solution)/shard_map/final/pallas_call | solution.py:39
  (1 shorter events, 0.0 us)
Async XLA Ops:
  2.2 7.5 %collective-permute-start = (f32[320,128]{1,0:T(8,128)S(1)}, f32[320,128]{1,0:T(8,128)S(1)}, u32[]{:S(2)}, u32[]{:S(2)}) collective-permute-start(f32[320,128]{1,0:T(8,128)S(1)} %get-tuple-element.27), channel_id=1, source_target_pairs={{1,2},{3,4},{5,6},{7,8},{9,10},{11,12},{13,14},{2,1},{4,3},{6,5},{... | collective-permute-start | bytes 491528 | tf_op jit(solution)/shard_map/ppermute | solution.py:253
  4.2 6.6 %collective-permute-start.1 = (f32[320,128]{1,0:T(8,128)S(1)}, f32[320,128]{1,0:T(8,128)S(1)}, u32[]{:S(2)}, u32[]{:S(2)}) collective-permute-start(f32[320,128]{1,0:T(8,128)S(1)} %get-tuple-element.28), channel_id=1, source_target_pairs={{0,1},{2,3},{4,5},{6,7},{8,9},{10,11},{12,13},{14,15},{1,0},{3,2},... | collective-permute-start | bytes 491528 | tf_op jit(solution)/shard_map/ppermute | solution.py:254
  10.9 8.6 %collective-permute-start.2 = (f32[6,40,128]{2,1,0:T(8,128)S(1)}, f32[6,40,128]{2,1,0:T(8,128)S(1)}, u32[]{:S(2)}, u32[]{:S(2)}) collective-permute-start(f32[6,40,128]{2,1,0:T(8,128)S(1)} %get-tuple-element.35), channel_id=1, source_target_pairs={{16,32},{48,64},{80,96},{112,128},{144,160},{176,192},{208,224},{2... | collective-permute-start | bytes 368648 | tf_op jit(solution)/shard_map/ppermute | solution.py:266
  11.6 9.7 %collective-permute-start.3 = (f32[6,40,128]{2,1,0:T(8,128)S(1)}, f32[6,40,128]{2,1,0:T(8,128)S(1)}, u32[]{:S(2)}, u32[]{:S(2)}) collective-permute-start(f32[6,40,128]{2,1,0:T(8,128)S(1)} %get-tuple-element.36), channel_id=1, source_target_pairs={{0,16},{32,48},{64,80},{96,112},{128,144},{160,176},{192,208},{224... | collective-permute-start | bytes 368648 | tf_op jit(solution)/shard_map/ppermute | solution.py:267

commit v5 on v4

--- a/solution.py
+++ b/solution.py
@@ -196,17 +196,7 @@
         copies[k] = total
 
 
-def middle_kernel(row, copies, before):
-    here = lax.axis_index("x")
-    total = jnp.zeros((COLS, MEMBERS), jnp.float32)
-    for k in range(row.shape[0]):
-        before[...] = jnp.where(k == here, total, before[...])
-        total = total + row[k]
-    for k in range(copies.shape[0]):
-        copies[k] = total
-
-
-def final_kernel(rows, before, inner_sums, edge_sums, offsets, edges, _end, potential_out, end_out, potential, sems):
+def final_kernel(totals, inner_sums, edge_sums, offsets, edges, _end, potential_out, end_out, potential, sems):
     copies = [
         pltpu.make_async_copy(edges.at[pl.ds(0, STEPS)], end_out.at[pl.ds(0, STEPS)], sems.at[0]),
         pltpu.make_async_copy(
@@ -215,10 +205,10 @@
     ]
     for copy in copies:
         copy.start()
-    here = lax.axis_index("y")
-    total = before[...]
-    for k in range(rows.shape[0]):
-        total = total + jnp.where(k < here, rows[k], 0.0)
+    here = lax.axis_index("y") * lax.axis_size("x") + lax.axis_index("x")
+    total = jnp.zeros((COLS, MEMBERS), jnp.float32)
+    for k in range(totals.shape[0]):
+        total = total + jnp.where(k < here, totals[k], 0.0)
     total = total * SCALE
     upper = total + offsets[1]
     for k in range(STEPS):
@@ -278,32 +268,23 @@
     )
     *_, edges, edge_sums, offsets, copies = call(
         edges_kernel,
-        [PADDED] * 3 + [in_vmem(2 * STEPS, COLS)] * 2 + [in_vmem(2, COLS), in_vmem(xs, COLS)],
+        [PADDED] * 3 + [in_vmem(2 * STEPS, COLS)] * 2 + [in_vmem(2, COLS), in_vmem(blocks, COLS)],
         "edges",
         (*padded, odd, even, inside),
         [VMEM] * 6,
         [VMEM] * 7,
         aliases=same,
     )
-    row = lax.all_to_all(copies, "x", 0, 0, tiled=True)
-    copies, before = call(
-        middle_kernel,
-        [in_vmem(ys, COLS), in_vmem(COLS)],
-        "middle",
-        (row,),
-        [VMEM],
-        [VMEM] * 2,
-    )
-    rows = lax.all_to_all(copies, "y", 0, 0, tiled=True)
+    totals = lax.all_to_all(copies, LAT, 0, 0, tiled=True)
     return call(
         final_kernel,
         [WHOLE] * 2,
         "final",
-        (rows, before, inner_sums, edge_sums, offsets, edges, end),
-        [VMEM] * 6 + [HBM],
+        (totals, inner_sums, edge_sums, offsets, edges, end),
+        [VMEM] * 5 + [HBM],
         [HBM] * 2,
         [in_vmem(ROWS, COLS), pltpu.SemaphoreType.DMA((2 + FINAL_PIECES,))],
-        aliases={6: 1},
+        aliases={5: 1},
     )
 
 

time: 48.2 us -> 48.9 us (1.015)
  blocking collectives: 25.5 us -> 26.2 us
    all_to_all x2 -> x1, blocking collectives: 25.5 us -> 26.2 us  [on_device(): totals = lax.all_to_all(copies, LAT, 0, 0, tiled=True)]
    pallas_call x6 -> x5, Pallas kernels: 4.61 us -> 4.68 us  [call(): pl.pallas_call(kernel, out_shape=outs, in_specs=specs, out_specs=out_spec...]
where the time goes in v5:
time: 48.9 us; the launch traced here: 48.7 us
  blocking collectives  26.2 us (54%)
  starting transfers between devices  14.3 us (29%)
  Pallas kernels  4.68 us (10%)
  waiting for transfers between devices  2.75 us (6%)
  between operations  0.71 us (1%)
    all_to_all x1, blocking collectives, on_device(): totals = lax.all_to_all(copies, LAT, 0, 0, tiled=True)  26.2 us
    ppermute x1, starting transfers between devices, on_device(): lax.ppermute(even, LAT, swap([(i, i + 1) for i in range(0, blocks, 2)]))  6.13 us
    ppermute x1, starting transfers between devices, on_device(): lax.ppermute(inner, LON, swap([(2 * z, 2 * z + 1) for z in range(chips)]))  5.59 us
    pallas_call x5, Pallas kernels, call(): pl.pallas_call(kernel, out_shape=outs, in_specs=specs, out_specs=out_spec...  4.68 us
    ppermute x1, starting transfers between devices, on_device(): lax.ppermute(outer, LON, swap([(2 * z + 1, 2 * z + 2) for z in range(chip...  1.92 us
    ppermute x1, waiting for transfers between devices, on_device(): lax.ppermute(even, LAT, swap([(i, i + 1) for i in range(0, blocks, 2)]))  1.75 us
    ppermute x1, waiting for transfers between devices, on_device(): lax.ppermute(inner, LON, swap([(2 * z, 2 * z + 1) for z in range(chips)]))  1 us
  transfers between devices with their start and end apart: 4, of which 2 were waited for; matrix products, arithmetic and copies ran while one was open for 0% of the time, Pallas kernels for 4%

profile of v5, /device:TPU:192, one launch (start us, length us, event | category | flops | bytes accessed | tf_op | source)
XLA Modules:
  0.0 48.7 jit_solution(16321360740983510877)
XLA Ops:
  0.6 1.6 %load.1 = (f32[40,56,128]{2,1,0:T(8,128)S(1)}, f32[40,56,128]{2,1,0:T(8,128)S(1)}, f32[40,56,128]{2,1,0:T(8,128)S(1)}, f32[320,128]{1,0:T(8,128)S(1)}, f32[320,128]{1,0:T(8,128)S(1)}) custom-call(f32[32,32,128]{2,1,0:T(8,128)} %pressure.1, f32[32,32,128]{2,1,0:T(8,128)} %earlier.1, f32[32,32,128]{2,1,0:T(8,128)} %speed.1), custom_call_target="tpu_custom_call" | custom-call | flops 100000 | tf_op jit(solution)/shard_map/load/pallas_call | solution.py:39
  2.2 1.9 %collective-permute-start = (f32[320,128]{1,0:T(8,128)S(1)}, f32[320,128]{1,0:T(8,128)S(1)}, u32[]{:S(2)}, u32[]{:S(2)}) collective-permute-start(f32[320,128]{1,0:T(8,128)S(1)} %get-tuple-element.25), channel_id=1, source_target_pairs={{1,2},{3,4},{5,6},{7,8},{9,10},{11,12},{13,14},{2,1},{4,3},{6,5},{... | collective-permute-start | bytes 491528 | tf_op jit(solution)/shard_map/ppermute | solution.py:243
  4.2 5.6 %collective-permute-start.1 = (f32[320,128]{1,0:T(8,128)S(1)}, f32[320,128]{1,0:T(8,128)S(1)}, u32[]{:S(2)}, u32[]{:S(2)}) collective-permute-start(f32[320,128]{1,0:T(8,128)S(1)} %get-tuple-element.26), channel_id=1, source_target_pairs={{0,1},{2,3},{4,5},{6,7},{8,9},{10,11},{12,13},{14,15},{1,0},{3,2},... | collective-permute-start | bytes 491528 | tf_op jit(solution)/shard_map/ppermute | solution.py:244
  9.8 0.0 collective-permute-done.outer
  9.8 1.0 %collective-permute-done.1.inner = f32[320,128]{1,0:T(8,128)S(1)} collective-permute-done((f32[320,128]{1,0:T(8,128)S(1)}, f32[320,128]{1,0:T(8,128)S(1)}, u32[]{:S(2)}, u32[]{:S(2)}) %collective-permute-start.1) | collective-permute-done | bytes 163872 | tf_op jit(solution)/shard_map/ppermute | solution.py:244
  10.8 0.1 columns.1
  10.9 0.7 %collective-permute-start.2 = (f32[6,40,128]{2,1,0:T(8,128)S(1)}, f32[6,40,128]{2,1,0:T(8,128)S(1)}, u32[]{:S(2)}, u32[]{:S(2)}) collective-permute-start(f32[6,40,128]{2,1,0:T(8,128)S(1)} %get-tuple-element.33), channel_id=1, source_target_pairs={{16,32},{48,64},{80,96},{112,128},{144,160},{176,192},{208,224},{2... | collective-permute-start | bytes 368648 | tf_op jit(solution)/shard_map/ppermute | solution.py:256
  11.6 6.1 %collective-permute-start.3 = (f32[6,40,128]{2,1,0:T(8,128)S(1)}, f32[6,40,128]{2,1,0:T(8,128)S(1)}, u32[]{:S(2)}, u32[]{:S(2)}) collective-permute-start(f32[6,40,128]{2,1,0:T(8,128)S(1)} %get-tuple-element.34), channel_id=1, source_target_pairs={{0,16},{32,48},{64,80},{96,112},{128,144},{160,176},{192,208},{224... | collective-permute-start | bytes 368648 | tf_op jit(solution)/shard_map/ppermute | solution.py:257
  17.7 1.8 %inner.1 = (f32[40,56,128]{2,1,0:T(8,128)S(1)}, f32[40,56,128]{2,1,0:T(8,128)S(1)}, f32[40,56,128]{2,1,0:T(8,128)S(1)}, f32[32,32,128]{2,1,0:T(8,128)}, f32[24,3...) custom-call(f32[40,56,128]{2,1,0:T(8,128)S(1)} %get-tuple-element.27._p, ...), custom_call_target="tpu_custom_call", output_to_operand_aliasing={{0}: (0, {}), {1}: (1, {}), {2}: (2, {})} | custom-call | flops 100000000 | tf_op jit(solution)/shard_map/inner/pallas_call | solution.py:39
  19.5 0.0 collective-permute-done.2.odd
  19.5 1.8 %collective-permute-done.3.even = f32[6,40,128]{2,1,0:T(8,128)S(1)} collective-permute-done((f32[6,40,128]{2,1,0:T(8,128)S(1)}, f32[6,40,128]{2,1,0:T(8,128)S(1)}, u32[]{:S(2)}, u32[]{:S(2)}) %collective-permute-start.3) | collective-permute-done | bytes 122912 | tf_op jit(solution)/shard_map/ppermute | solution.py:257
  21.3 0.2 edges.1
  21.5 26.2 %all_to_all.5.totals = f32[32,32,128]{2,1,0:T(8,128)S(1)} all-to-all(f32[32,32,128]{2,1,0:T(8,128)S(1)} %get-tuple-element.36), channel_id=1, replica_groups=mesh['y'=8,'x'=4,'z'=8,'core'=2] {'y','x'}, dimensions={0} | all-to-all | bytes 1048576 | tf_op jit(solution)/shard_map/all_to_all | solution.py:278
  47.7 0.9 %final.1 = (f32[32,32,128]{2,1,0:T(8,128)}, f32[32,32,128]{2,1,0:T(8,128)}) custom-call(f32[32,32,128]{2,1,0:T(8,128)S(1)} %all_to_all.5.totals, f32[24,32,128]{2,1,0:T(8,128)S(1)} %get-tuple-element.37.inner_sums, f32[8,32,128]{2,1,0:T(8,128)S(1)} %get-tuple-element.38.edge_sums, ...), custom_call_target="tpu_custom_call", output_to_operand_aliasing={{1}: (5, {})} | custom-call | flops 100000 | tf_op jit(solution)/shard_map/final/pallas_call | solution.py:39
Async XLA Ops:
  2.2 7.5 %collective-permute-start = (f32[320,128]{1,0:T(8,128)S(1)}, f32[320,128]{1,0:T(8,128)S(1)}, u32[]{:S(2)}, u32[]{:S(2)}) collective-permute-start(f32[320,128]{1,0:T(8,128)S(1)} %get-tuple-element.25), channel_id=1, source_target_pairs={{1,2},{3,4},{5,6},{7,8},{9,10},{11,12},{13,14},{2,1},{4,3},{6,5},{... | collective-permute-start | bytes 491528 | tf_op jit(solution)/shard_map/ppermute | solution.py:243
  4.2 6.6 %collective-permute-start.1 = (f32[320,128]{1,0:T(8,128)S(1)}, f32[320,128]{1,0:T(8,128)S(1)}, u32[]{:S(2)}, u32[]{:S(2)}) collective-permute-start(f32[320,128]{1,0:T(8,128)S(1)} %get-tuple-element.26), channel_id=1, source_target_pairs={{0,1},{2,3},{4,5},{6,7},{8,9},{10,11},{12,13},{14,15},{1,0},{3,2},... | collective-permute-start | bytes 491528 | tf_op jit(solution)/shard_map/ppermute | solution.py:244
  10.9 8.6 %collective-permute-start.2 = (f32[6,40,128]{2,1,0:T(8,128)S(1)}, f32[6,40,128]{2,1,0:T(8,128)S(1)}, u32[]{:S(2)}, u32[]{:S(2)}) collective-permute-start(f32[6,40,128]{2,1,0:T(8,128)S(1)} %get-tuple-element.33), channel_id=1, source_target_pairs={{16,32},{48,64},{80,96},{112,128},{144,160},{176,192},{208,224},{2... | collective-permute-start | bytes 368648 | tf_op jit(solution)/shard_map/ppermute | solution.py:256
  11.6 9.7 %collective-permute-start.3 = (f32[6,40,128]{2,1,0:T(8,128)S(1)}, f32[6,40,128]{2,1,0:T(8,128)S(1)}, u32[]{:S(2)}, u32[]{:S(2)}) collective-permute-start(f32[6,40,128]{2,1,0:T(8,128)S(1)} %get-tuple-element.34), channel_id=1, source_target_pairs={{0,16},{32,48},{64,80},{96,112},{128,144},{160,176},{192,208},{224... | collective-permute-start | bytes 368648 | tf_op jit(solution)/shard_map/ppermute | solution.py:257

commit v6 on v4

--- a/solution.py
+++ b/solution.py
@@ -18,6 +18,9 @@
 FINAL_PIECES = 4
 INSIDE = ROWS - 2 * STEPS
 SCALE = 1.0 / 1024
+REACHES = (3, 2, 2, 1, 2, 0)
+PLACES = tuple(sum(COLS + 2 * reach for reach in REACHES[:k]) for k in range(6))
+ROW_CELLS = PLACES[-1] + COLS + 2 * REACHES[-1]
 LAT = ("y", "x")
 LON = ("z", "core")
 
@@ -62,8 +65,7 @@
             slot += 1
 
 
-def message_to_columns(padded, message, at_start):
-    slot = 0
+def message_to_columns(padded, message, at_start, slot=0):
     for ref, depth in zip(padded, DEPTHS):
         first = jnp.where(at_start, -depth, COLS)
         for k in range(depth):
@@ -76,19 +78,23 @@
     first, second, third = (HALO + jnp.where(at_start, k, ROWS - 1 - k) for k in range(3))
     cells = slice(LEFT - HALO, LEFT - HALO + WIDE)
     beyond = speed[second, cells, :] * later_row(now, before, speed, third, LEFT - HALO, WIDE)
-    message[0] = now[first, cells, :]
-    message[1] = now[second, cells, :] - beyond
-    message[2] = before[first, cells, :] - speed[first, cells, :] * beyond
-    message[3] = later_row(now, before, speed, second, LEFT - HALO, WIDE)
-    message[4] = speed[first, cells, :]
-    message[5] = speed[second, cells, :]
+    values = (
+        now[first, cells, :],
+        now[second, cells, :] - beyond,
+        before[first, cells, :] - speed[first, cells, :] * beyond,
+        later_row(now, before, speed, second, LEFT - HALO, WIDE),
+        speed[first, cells, :],
+        speed[second, cells, :],
+    )
+    for value, at, reach in zip(values, PLACES, REACHES):
+        message[at : at + COLS + 2 * reach] = value[HALO - reach : HALO + COLS + reach]
 
 
 def message_to_rows(padded, message, at_start):
-    for k in range(2):
-        row = HALO + jnp.where(at_start, -1 - k, ROWS + k)
-        for slot, ref in enumerate(padded):
-            ref[row, LEFT - HALO : LEFT - HALO + WIDE, :] = message[2 * slot + k]
+    for slot, (at, reach) in enumerate(zip(PLACES, REACHES)):
+        row = HALO + jnp.where(at_start, -1 - slot % 2, ROWS + slot % 2)
+        width = COLS + 2 * reach
+        padded[slot // 2][row, LEFT - reach : LEFT + COLS + reach, :] = message[at : at + width]
 
 
 def load_kernel(pressure, earlier, speed, *refs):
@@ -116,7 +122,7 @@
     padded, (odd, even) = refs[:3], refs[3:5]
     first_core = lax.axis_index("core") == 0
     message_to_columns(padded, outer, first_core)
-    message_to_columns(padded, inner, jnp.logical_not(first_core))
+    message_to_columns(padded, inner, jnp.logical_not(first_core), jnp.where(first_core, DEEP, 0))
     odd_x = lax.axis_index("x") % 2 == 1
     rows_to_message(padded, odd, jnp.logical_not(odd_x))
     rows_to_message(padded, even, odd_x)
@@ -251,11 +257,11 @@
     chips, ys, xs = (lax.axis_size(name) for name in ("z", "y", "x"))
     swap = lambda pairs: pairs + [(b, a) for a, b in pairs]
     outer = lax.ppermute(outer, LON, swap([(2 * z + 1, 2 * z + 2) for z in range(chips - 1)]))
-    inner = lax.ppermute(inner, LON, swap([(2 * z, 2 * z + 1) for z in range(chips)]))
+    inner = lax.all_gather(inner, "core", axis=0, tiled=True)
     same = {0: 0, 1: 1, 2: 2}
     *padded, odd, even = call(
         columns_kernel,
-        [PADDED] * 3 + [in_vmem(6, WIDE)] * 2,
+        [PADDED] * 3 + [in_vmem(ROW_CELLS)] * 2,
         "columns",
         (*padded, outer, inner),
         [VMEM] * 5,

time: 48.2 us -> 47.5 us (0.985)
  blocking collectives: 25.5 us -> 31.4 us
  starting transfers between devices: 14.3 us -> 8.72 us
  waiting for transfers between devices: 2.75 us -> 1.66 us
    ppermute x1 -> x0, starting transfers between devices: 5.59 us -> none  [on_device(): lax.ppermute(inner, LON, swap([(2 * z, 2 * z + 1) for z in range(chips)]))]
    all_gather x0 -> x1, blocking collectives: none -> 5.36 us  [on_device(): inner = lax.all_gather(inner, 'core', axis=0, tiled=True)]
    ppermute x1 -> x0, waiting for transfers between devices: 1 us -> none  [on_device(): lax.ppermute(inner, LON, swap([(2 * z, 2 * z + 1) for z in range(chips)]))]
    all_to_all x1, blocking collectives: 9.7 us -> 10.3 us  [on_device(): row = lax.all_to_all(copies, 'x', 0, 0, tiled=True)]
  transfers between devices with their start and end apart: 4 -> 3, of which waited for: 2 -> 1; matrix products, arithmetic and copies ran while one was open for 0% -> 0% of each run, Pallas kernels for 4% -> 4%
where the time goes in v6:
time: 47.5 us; the launch traced here: 47.2 us
  blocking collectives  31.4 us (66%)
  starting transfers between devices  8.72 us (18%)
  Pallas kernels  4.73 us (10%)
  waiting for transfers between devices  1.66 us (3%)
  between operations  0.69 us (1%)
    all_to_all x1, blocking collectives, on_device(): rows = lax.all_to_all(copies, 'y', 0, 0, tiled=True)  15.8 us
    all_to_all x1, blocking collectives, on_device(): row = lax.all_to_all(copies, 'x', 0, 0, tiled=True)  10.3 us
    ppermute x1, starting transfers between devices, on_device(): lax.ppermute(even, LAT, swap([(i, i + 1) for i in range(0, blocks, 2)]))  6.13 us
    all_gather x1, blocking collectives, on_device(): inner = lax.all_gather(inner, 'core', axis=0, tiled=True)  5.36 us
    pallas_call x6, Pallas kernels, call(): pl.pallas_call(kernel, out_shape=outs, in_specs=specs, out_specs=out_spec...  4.73 us
    ppermute x1, starting transfers between devices, on_device(): lax.ppermute(outer, LON, swap([(2 * z + 1, 2 * z + 2) for z in range(chip...  1.92 us
    ppermute x1, waiting for transfers between devices, on_device(): lax.ppermute(even, LAT, swap([(i, i + 1) for i in range(0, blocks, 2)]))  1.66 us
  transfers between devices with their start and end apart: 3, of which 1 were waited for; matrix products, arithmetic and copies ran while one was open for 0% of the time, Pallas kernels for 4%

profile of v6, /device:TPU:192, one launch (start us, length us, event | category | flops | bytes accessed | tf_op | source)
XLA Modules:
  0.0 47.2 jit_solution(5558993530663350498)
XLA Ops:
  0.6 1.6 %load.1 = (f32[40,56,128]{2,1,0:T(8,128)S(1)}, f32[40,56,128]{2,1,0:T(8,128)S(1)}, f32[40,56,128]{2,1,0:T(8,128)S(1)}, f32[320,128]{1,0:T(8,128)S(1)}, f32[320,128]{1,0:T(8,128)S(1)}) custom-call(f32[32,32,128]{2,1,0:T(8,128)} %pressure.1, f32[32,32,128]{2,1,0:T(8,128)} %earlier.1, f32[32,32,128]{2,1,0:T(8,128)} %speed.1), custom_call_target="tpu_custom_call" | custom-call | flops 100000 | tf_op jit(solution)/shard_map/load/pallas_call | solution.py:42
  2.2 1.9 %collective-permute-start = (f32[320,128]{1,0:T(8,128)S(1)}, f32[320,128]{1,0:T(8,128)S(1)}, u32[]{:S(2)}, u32[]{:S(2)}) collective-permute-start(f32[320,128]{1,0:T(8,128)S(1)} %get-tuple-element.27), channel_id=1, source_target_pairs={{1,2},{3,4},{5,6},{7,8},{9,10},{11,12},{13,14},{2,1},{4,3},{6,5},{... | collective-permute-start | bytes 491528 | tf_op jit(solution)/shard_map/ppermute | solution.py:259
  4.2 5.4 %all_gather.3.inner = f32[640,128]{1,0:T(8,128)S(1)} all-gather(f32[320,128]{1,0:T(8,128)S(1)} %get-tuple-element.28), channel_id=1, replica_groups=mesh['y'=8,'x'=4,'z'=8,'core'=2] {'core'}, dimensions={0}, use_global_device_ids=true | all-gather | bytes 491520 | tf_op jit(solution)/shard_map/all_gather | solution.py:260
  9.5 0.0 collective-permute-done.outer
  9.5 0.1 columns.1
  9.6 0.7 %collective-permute-start.1 = (f32[212,128]{1,0:T(8,128)S(1)}, f32[212,128]{1,0:T(8,128)S(1)}, u32[]{:S(2)}, u32[]{:S(2)}) collective-permute-start(f32[212,128]{1,0:T(8,128)S(1)} %get-tuple-element.35), channel_id=1, source_target_pairs={{16,32},{48,64},{80,96},{112,128},{144,160},{176,192},{208,224},{2... | collective-permute-start | bytes 325640 | tf_op jit(solution)/shard_map/ppermute | solution.py:272
  10.3 6.1 %collective-permute-start.2 = (f32[212,128]{1,0:T(8,128)S(1)}, f32[212,128]{1,0:T(8,128)S(1)}, u32[]{:S(2)}, u32[]{:S(2)}) collective-permute-start(f32[212,128]{1,0:T(8,128)S(1)} %get-tuple-element.36), channel_id=1, source_target_pairs={{0,16},{32,48},{64,80},{96,112},{128,144},{160,176},{192,208},{224... | collective-permute-start | bytes 325640 | tf_op jit(solution)/shard_map/ppermute | solution.py:273
  16.5 1.9 %inner.1 = (f32[40,56,128]{2,1,0:T(8,128)S(1)}, f32[40,56,128]{2,1,0:T(8,128)S(1)}, f32[40,56,128]{2,1,0:T(8,128)S(1)}, f32[32,32,128]{2,1,0:T(8,128)}, f32[24,3...) custom-call(f32[40,56,128]{2,1,0:T(8,128)S(1)} %get-tuple-element.29._p, ...), custom_call_target="tpu_custom_call", output_to_operand_aliasing={{0}: (0, {}), {1}: (1, {}), {2}: (2, {})} | custom-call | flops 100000000 | tf_op jit(solution)/shard_map/inner/pallas_call | solution.py:42
  18.3 0.0 collective-permute-done.1.odd
  18.4 1.7 %collective-permute-done.2.even = f32[212,128]{1,0:T(8,128)S(1)} collective-permute-done((f32[212,128]{1,0:T(8,128)S(1)}, f32[212,128]{1,0:T(8,128)S(1)}, u32[]{:S(2)}, u32[]{:S(2)}) %collective-permute-start.2) | collective-permute-done | bytes 108576 | tf_op jit(solution)/shard_map/ppermute | solution.py:273
  20.0 0.2 edges.1
  20.3 10.3 %all_to_all.10.row = f32[4,32,128]{2,1,0:T(8,128)S(1)} all-to-all(f32[4,32,128]{2,1,0:T(8,128)S(1)} %get-tuple-element.38), channel_id=1, replica_groups=mesh['y'=8,'x'=4,'z'=8,'core'=2] {'x'}, dimensions={0} | all-to-all | bytes 131072 | tf_op jit(solution)/shard_map/all_to_all | solution.py:294
  30.5 15.8 %all_to_all.11.rows = f32[8,32,128]{2,1,0:T(8,128)S(1)} all-to-all(f32[8,32,128]{2,1,0:T(8,128)S(1)} %get-tuple-element.39), channel_id=1, replica_groups=mesh['y'=8,'x'=4,'z'=8,'core'=2] {'y'}, dimensions={0} | all-to-all | bytes 262144 | tf_op jit(solution)/shard_map/all_to_all | solution.py:303
  46.3 0.9 %final.1 = (f32[32,32,128]{2,1,0:T(8,128)}, f32[32,32,128]{2,1,0:T(8,128)}) custom-call(f32[8,32,128]{2,1,0:T(8,128)S(1)} %all_to_all.11.rows, f32[32,128]{1,0:T(8,128)S(1)} %get-tuple-element.40.before, f32[24,32,128]{2,1,0:T(8,128)S(1)} %get-tuple-element.41.inner_sums, ...), custom_call_target="tpu_custom_call", output_to_operand_aliasing={{1}: (6, {})} | custom-call | flops 100000 | tf_op jit(solution)/shard_map/final/pallas_call | solution.py:42
  (1 shorter events, 0.0 us)
Async XLA Ops:
  2.2 7.3 %collective-permute-start = (f32[320,128]{1,0:T(8,128)S(1)}, f32[320,128]{1,0:T(8,128)S(1)}, u32[]{:S(2)}, u32[]{:S(2)}) collective-permute-start(f32[320,128]{1,0:T(8,128)S(1)} %get-tuple-element.27), channel_id=1, source_target_pairs={{1,2},{3,4},{5,6},{7,8},{9,10},{11,12},{13,14},{2,1},{4,3},{6,5},{... | collective-permute-start | bytes 491528 | tf_op jit(solution)/shard_map/ppermute | solution.py:259
  9.6 8.7 %collective-permute-start.1 = (f32[212,128]{1,0:T(8,128)S(1)}, f32[212,128]{1,0:T(8,128)S(1)}, u32[]{:S(2)}, u32[]{:S(2)}) collective-permute-start(f32[212,128]{1,0:T(8,128)S(1)} %get-tuple-element.35), channel_id=1, source_target_pairs={{16,32},{48,64},{80,96},{112,128},{144,160},{176,192},{208,224},{2... | collective-permute-start | bytes 325640 | tf_op jit(solution)/shard_map/ppermute | solution.py:272
  10.3 9.7 %collective-permute-start.2 = (f32[212,128]{1,0:T(8,128)S(1)}, f32[212,128]{1,0:T(8,128)S(1)}, u32[]{:S(2)}, u32[]{:S(2)}) collective-permute-start(f32[212,128]{1,0:T(8,128)S(1)} %get-tuple-element.36), channel_id=1, source_target_pairs={{0,16},{32,48},{64,80},{96,112},{128,144},{160,176},{192,208},{224... | collective-permute-start | bytes 325640 | tf_op jit(solution)/shard_map/ppermute | solution.py:273

commit v7 on v6

--- a/solution.py
+++ b/solution.py
@@ -14,7 +14,7 @@
 WIDE = COLS + 2 * HALO
 DEPTHS = (HALO, HALO - 1, HALO - 1)
 DEEP = sum(DEPTHS)
-PIECES = 4
+TILE = 8
 FINAL_PIECES = 4
 INSIDE = ROWS - 2 * STEPS
 SCALE = 1.0 / 1024
@@ -97,25 +97,36 @@
         padded[slot // 2][row, LEFT - reach : LEFT + COLS + reach, :] = message[at : at + width]
 
 
-def load_kernel(pressure, earlier, speed, *refs):
-    padded, (outer, inner), sems = refs[:3], refs[3:5], refs[5]
-    piece = ROWS // PIECES
+def outer_kernel(pressure, earlier, speed, message, tiles, sems):
+    first_core = lax.axis_index("core") == 0
+    first = pl.multiple_of(jnp.where(first_core, 0, COLS - TILE), TILE)
     copies = [
-        pltpu.make_async_copy(
-            source.at[pl.ds(k * piece, piece)],
-            target.at[pl.ds(HALO + k * piece, piece), pl.ds(LEFT, COLS), :],
-            sems.at[i, k],
-        )
-        for i, (source, target) in enumerate(zip((pressure, earlier, speed), padded))
-        for k in range(PIECES)
+        pltpu.make_async_copy(source.at[:, pl.ds(first, TILE), :], tiles.at[i], sems.at[i])
+        for i, source in enumerate((pressure, earlier, speed))
     ]
     for copy in copies:
         copy.start()
-    for copy in copies:
-        copy.wait()
-    first_core = lax.axis_index("core") == 0
-    columns_to_message(padded, outer, first_core)
-    columns_to_message(padded, inner, jnp.logical_not(first_core))
+    slot = 0
+    for i, depth in enumerate(DEPTHS):
+        copies[i].wait()
+        cells = tiles.at[i].reshape(ROWS * TILE, MEMBERS)
+        start = jnp.where(first_core, 0, TILE - depth)
+        for k in range(depth):
+            message[pl.ds(slot * ROWS, ROWS), :] = cells[pl.ds(start + k, ROWS, stride=TILE), :]
+            slot += 1
+
+
+def load_kernel(pressure, earlier, speed, *refs):
+    padded, inner = refs[:3], refs[3]
+    for source, target in zip((pressure, earlier, speed), padded):
+
+        def some(i, _, source=source, target=target):
+            for k in range(4):
+                target[HALO + 4 * i + k, LEFT : LEFT + COLS, :] = source[4 * i + k]
+            return 0
+
+        lax.fori_loop(0, ROWS // 4, some, 0)
+    columns_to_message(padded, inner, lax.axis_index("core") != 0)
 
 
 def columns_kernel(_p, _e, _s, outer, inner, *refs):
@@ -245,18 +256,27 @@
 
 
 def on_device(pressure, earlier, speed_square):
-    *padded, outer, inner = call(
-        load_kernel,
-        [PADDED] * 3 + [in_vmem(DEEP * ROWS)] * 2,
-        "load",
-        [pltpu.with_memory_space_constraint(a, pltpu.HBM) for a in (pressure, earlier, speed_square)],
+    args = [pltpu.with_memory_space_constraint(a, pltpu.HBM) for a in (pressure, earlier, speed_square)]
+    outer = call(
+        outer_kernel,
+        in_vmem(DEEP * ROWS),
+        "outer",
+        args,
         [HBM] * 3,
-        [VMEM] * 5,
-        [pltpu.SemaphoreType.DMA((3, PIECES))],
+        VMEM,
+        [in_vmem(3, ROWS, TILE), pltpu.SemaphoreType.DMA((3,))],
     )
     chips, ys, xs = (lax.axis_size(name) for name in ("z", "y", "x"))
     swap = lambda pairs: pairs + [(b, a) for a, b in pairs]
     outer = lax.ppermute(outer, LON, swap([(2 * z + 1, 2 * z + 2) for z in range(chips - 1)]))
+    *padded, inner = call(
+        load_kernel,
+        [PADDED] * 3 + [in_vmem(DEEP * ROWS)],
+        "load",
+        [pltpu.with_memory_space_constraint(a, pltpu.VMEM) for a in (pressure, earlier, speed_square)],
+        [VMEM] * 3,
+        [VMEM] * 4,
+    )
     inner = lax.all_gather(inner, "core", axis=0, tiled=True)
     same = {0: 0, 1: 1, 2: 2}
     *padded, odd, even = call(

time: 47.5 us -> 47.2 us (level)
    pallas_call x6 -> x7, Pallas kernels: 4.73 us -> 4.38 us  [call(): pl.pallas_call(kernel, out_shape=outs, in_specs=specs, out_specs=out_spec...]
where the time goes in v7:
time: 47.2 us; the launch traced here: 46.9 us
  blocking collectives  31.1 us (66%)
  starting transfers between devices  8.72 us (18%)
  Pallas kernels  4.38 us (9%)
  waiting for transfers between devices  1.98 us (4%)
  between operations  0.75 us (2%)
    all_to_all x1, blocking collectives, on_device(): rows = lax.all_to_all(copies, 'y', 0, 0, tiled=True)  15.8 us
    all_to_all x1, blocking collectives, on_device(): row = lax.all_to_all(copies, 'x', 0, 0, tiled=True)  9.93 us
    ppermute x1, starting transfers between devices, on_device(): lax.ppermute(even, LAT, swap([(i, i + 1) for i in range(0, blocks, 2)]))  6.13 us
    all_gather x1, blocking collectives, on_device(): inner = lax.all_gather(inner, 'core', axis=0, tiled=True)  5.36 us
    pallas_call x7, Pallas kernels, call(): pl.pallas_call(kernel, out_shape=outs, in_specs=specs, out_specs=out_spec...  4.38 us
    ppermute x1, waiting for transfers between devices, on_device(): lax.ppermute(even, LAT, swap([(i, i + 1) for i in range(0, blocks, 2)]))  1.97 us
    ppermute x1, starting transfers between devices, on_device(): lax.ppermute(outer, LON, swap([(2 * z + 1, 2 * z + 2) for z in range(chip...  1.92 us
  transfers between devices with their start and end apart: 3, of which 1 were waited for; matrix products, arithmetic and copies ran while one was open for 0% of the time, Pallas kernels for 4%

profile of v7, /device:TPU:192, one launch (start us, length us, event | category | flops | bytes accessed | tf_op | source)
XLA Modules:
  0.0 46.9 jit_solution(5112489924282471676)
XLA Ops:
  0.6 0.0 copy-start.2
  0.6 0.0 copy-start.1
  0.6 0.0 copy-start
  0.7 1.2 %outer.1 = f32[320,128]{1,0:T(8,128)S(1)} custom-call(f32[32,32,128]{2,1,0:T(8,128)} %pressure.3, f32[32,32,128]{2,1,0:T(8,128)} %earlier.3, f32[32,32,128]{2,1,0:T(8,128)} %speed.3), custom_call_target="tpu_custom_call" | custom-call | flops 100000 | tf_op jit(solution)/shard_map/outer/pallas_call | solution.py:42
  1.9 1.9 %collective-permute-start = (f32[320,128]{1,0:T(8,128)S(1)}, f32[320,128]{1,0:T(8,128)S(1)}, u32[]{:S(2)}, u32[]{:S(2)}) collective-permute-start(f32[320,128]{1,0:T(8,128)S(1)} %outer.1), channel_id=1, source_target_pairs={{1,2},{3,4},{5,6},{7,8},{9,10},{11,12},{13,14},{2,1},{4,3},{6,5},{... | collective-permute-start | bytes 491528 | tf_op jit(solution)/shard_map/ppermute | solution.py:271
  3.8 0.0 copy-done.2
  3.8 0.0 copy-done.1
  3.8 0.0 copy-done
  3.8 0.2 load.1
  4.0 5.4 %all_gather.3.inner = f32[640,128]{1,0:T(8,128)S(1)} all-gather(f32[320,128]{1,0:T(8,128)S(1)} %get-tuple-element.26), channel_id=1, replica_groups=mesh['y'=8,'x'=4,'z'=8,'core'=2] {'core'}, dimensions={0}, use_global_device_ids=true | all-gather | bytes 491520 | tf_op jit(solution)/shard_map/all_gather | solution.py:280
  9.4 0.0 collective-permute-done.outer
  9.4 0.1 columns.1
  9.5 0.7 %collective-permute-start.1 = (f32[212,128]{1,0:T(8,128)S(1)}, f32[212,128]{1,0:T(8,128)S(1)}, u32[]{:S(2)}, u32[]{:S(2)}) collective-permute-start(f32[212,128]{1,0:T(8,128)S(1)} %get-tuple-element.33), channel_id=1, source_target_pairs={{16,32},{48,64},{80,96},{112,128},{144,160},{176,192},{208,224},{2... | collective-permute-start | bytes 325640 | tf_op jit(solution)/shard_map/ppermute | solution.py:292
  10.2 6.1 %collective-permute-start.2 = (f32[212,128]{1,0:T(8,128)S(1)}, f32[212,128]{1,0:T(8,128)S(1)}, u32[]{:S(2)}, u32[]{:S(2)}) collective-permute-start(f32[212,128]{1,0:T(8,128)S(1)} %get-tuple-element.34), channel_id=1, source_target_pairs={{0,16},{32,48},{64,80},{96,112},{128,144},{160,176},{192,208},{224... | collective-permute-start | bytes 325640 | tf_op jit(solution)/shard_map/ppermute | solution.py:293
  16.3 1.8 %inner.1 = (f32[40,56,128]{2,1,0:T(8,128)S(1)}, f32[40,56,128]{2,1,0:T(8,128)S(1)}, f32[40,56,128]{2,1,0:T(8,128)S(1)}, f32[32,32,128]{2,1,0:T(8,128)}, f32[24,3...) custom-call(f32[40,56,128]{2,1,0:T(8,128)S(1)} %get-tuple-element.27._p, ...), custom_call_target="tpu_custom_call", output_to_operand_aliasing={{0}: (0, {}), {1}: (1, {}), {2}: (2, {})} | custom-call | flops 100000000 | tf_op jit(solution)/shard_map/inner/pallas_call | solution.py:42
  18.1 0.0 collective-permute-done.1.odd
  18.1 2.0 %collective-permute-done.2.even = f32[212,128]{1,0:T(8,128)S(1)} collective-permute-done((f32[212,128]{1,0:T(8,128)S(1)}, f32[212,128]{1,0:T(8,128)S(1)}, u32[]{:S(2)}, u32[]{:S(2)}) %collective-permute-start.2) | collective-permute-done | bytes 108576 | tf_op jit(solution)/shard_map/ppermute | solution.py:293
  20.1 0.2 edges.1
  20.3 9.9 %all_to_all.10.row = f32[4,32,128]{2,1,0:T(8,128)S(1)} all-to-all(f32[4,32,128]{2,1,0:T(8,128)S(1)} %get-tuple-element.36), channel_id=1, replica_groups=mesh['y'=8,'x'=4,'z'=8,'core'=2] {'x'}, dimensions={0} | all-to-all | bytes 131072 | tf_op jit(solution)/shard_map/all_to_all | solution.py:314
  30.2 15.8 %all_to_all.11.rows = f32[8,32,128]{2,1,0:T(8,128)S(1)} all-to-all(f32[8,32,128]{2,1,0:T(8,128)S(1)} %get-tuple-element.37), channel_id=1, replica_groups=mesh['y'=8,'x'=4,'z'=8,'core'=2] {'y'}, dimensions={0} | all-to-all | bytes 262144 | tf_op jit(solution)/shard_map/all_to_all | solution.py:323
  46.0 0.9 %final.1 = (f32[32,32,128]{2,1,0:T(8,128)}, f32[32,32,128]{2,1,0:T(8,128)}) custom-call(f32[8,32,128]{2,1,0:T(8,128)S(1)} %all_to_all.11.rows, f32[32,128]{1,0:T(8,128)S(1)} %get-tuple-element.38.before, f32[24,32,128]{2,1,0:T(8,128)S(1)} %get-tuple-element.39.inner_sums, ...), custom_call_target="tpu_custom_call", output_to_operand_aliasing={{1}: (6, {})} | custom-call | flops 100000 | tf_op jit(solution)/shard_map/final/pallas_call | solution.py:42
  (1 shorter events, 0.0 us)
Async XLA Ops:
  0.6 3.2 %copy-start.2 = (f32[32,32,128]{2,1,0:T(8,128)S(1)}, f32[32,32,128]{2,1,0:T(8,128)}, u32[]{:S(2)}) copy-start(f32[32,32,128]{2,1,0:T(8,128)} %speed.3) | copy-start | bytes 1572868
  0.6 3.2 %copy-start.1 = (f32[32,32,128]{2,1,0:T(8,128)S(1)}, f32[32,32,128]{2,1,0:T(8,128)}, u32[]{:S(2)}) copy-start(f32[32,32,128]{2,1,0:T(8,128)} %earlier.3) | copy-start | bytes 1572868
  0.6 3.2 %copy-start = (f32[32,32,128]{2,1,0:T(8,128)S(1)}, f32[32,32,128]{2,1,0:T(8,128)}, u32[]{:S(2)}) copy-start(f32[32,32,128]{2,1,0:T(8,128)} %pressure.3) | copy-start | bytes 1572868
  1.9 7.5 %collective-permute-start = (f32[320,128]{1,0:T(8,128)S(1)}, f32[320,128]{1,0:T(8,128)S(1)}, u32[]{:S(2)}, u32[]{:S(2)}) collective-permute-start(f32[320,128]{1,0:T(8,128)S(1)} %outer.1), channel_id=1, source_target_pairs={{1,2},{3,4},{5,6},{7,8},{9,10},{11,12},{13,14},{2,1},{4,3},{6,5},{... | collective-permute-start | bytes 491528 | tf_op jit(solution)/shard_map/ppermute | solution.py:271
  9.5 8.6 %collective-permute-start.1 = (f32[212,128]{1,0:T(8,128)S(1)}, f32[212,128]{1,0:T(8,128)S(1)}, u32[]{:S(2)}, u32[]{:S(2)}) collective-permute-start(f32[212,128]{1,0:T(8,128)S(1)} %get-tuple-element.33), channel_id=1, source_target_pairs={{16,32},{48,64},{80,96},{112,128},{144,160},{176,192},{208,224},{2... | collective-permute-start | bytes 325640 | tf_op jit(solution)/shard_map/ppermute | solution.py:292
  10.2 9.9 %collective-permute-start.2 = (f32[212,128]{1,0:T(8,128)S(1)}, f32[212,128]{1,0:T(8,128)S(1)}, u32[]{:S(2)}, u32[]{:S(2)}) collective-permute-start(f32[212,128]{1,0:T(8,128)S(1)} %get-tuple-element.34), channel_id=1, source_target_pairs={{0,16},{32,48},{64,80},{96,112},{128,144},{160,176},{192,208},{224... | collective-permute-start | bytes 325640 | tf_op jit(solution)/shard_map/ppermute | solution.py:293

commit v8 on v7

v8 whole, which is shorter than its diff:
```python
import jax
import jax.numpy as jnp
from jax import lax
from jax.experimental import pallas as pl
from jax.experimental.pallas import tpu as pltpu
from jax.sharding import Mesh, PartitionSpec as P

STEPS = 4
ROWS, COLS, MEMBERS = 32, 32, 128
PITCH = 56
LEFT = 8
HALO = STEPS
TALL = ROWS + 2 * HALO
WIDE = COLS + 2 * HALO
DEPTHS = (HALO, HALO - 1, HALO - 1)
DEEP = sum(DEPTHS)
TILE = 8
FINAL_PIECES = 4
INSIDE = ROWS - 2 * STEPS
SCALE = 1.0 / 1024
REACHES = (3, 2, 2, 1, 2, 0)
PLACES = tuple(sum(COLS + 2 * reach for reach in REACHES[:k]) for k in range(6))
ROW_CELLS = -(-(PLACES[-1] + COLS + 2 * REACHES[-1]) // 8) * 8
X = ("xh", "xl")
LAT = ("y", *X)
LON = ("z", "core")

HBM = pl.BlockSpec(memory_space=pltpu.HBM)
VMEM = pl.BlockSpec(memory_space=pltpu.VMEM)
WHOLE = pltpu.HBM((ROWS, COLS, MEMBERS), jnp.float32)
PADDED = pltpu.VMEM((TALL, PITCH, MEMBERS), jnp.float32)
RAW = pltpu.VMEM((2 * HALO, PITCH, MEMBERS), jnp.float32)


def in_vmem(*shape):
    return pltpu.VMEM((*shape, MEMBERS), jnp.float32)


def flat(ref):
    return ref.reshape(ref.shape[0] * ref.shape[1], MEMBERS)


def call(kernel, outs, name, args, specs, out_specs, scratch=(), aliases=None, flops=10**5):
    return pl.pallas_call(
        kernel,
        out_shape=outs,
        in_specs=specs,
        out_specs=out_specs,
        scratch_shapes=scratch,
        input_output_aliases=aliases or {},
        name=name,
        cost_estimate=pl.CostEstimate(flops=flops, bytes_accessed=0, transcendentals=0),
        compiler_params=pltpu.CompilerParams(vmem_limit_bytes=16 * 2**20),
    )(*args)


def cell(row, col):
    return (row + HALO) * PITCH + LEFT + col


def columns_to_message(padded, message, at_start):
    slot = 0
    for ref, depth in zip(padded, DEPTHS):
        first = jnp.where(at_start, 0, COLS - depth)
        for k in range(depth):
            message[pl.ds(slot * ROWS, ROWS), :] = flat(ref)[pl.ds(cell(0, first + k), ROWS, stride=PITCH), :]
            slot += 1


def message_to_columns(padded, raw, message, at_start, slot=0):
    for ref, ends, depth in zip(padded, raw, DEPTHS):
        first = jnp.where(at_start, -depth, COLS)
        for k in range(depth):
            at = slot * ROWS
            flat(ref)[pl.ds(cell(0, first + k), ROWS, stride=PITCH), :] = message[pl.ds(at, ROWS), :]
            for row, source in ((0, at), (HALO, at + ROWS - HALO)):
                place = pl.ds(row * PITCH + LEFT + first + k, HALO, stride=PITCH)
                flat(ends)[place, :] = message[pl.ds(source, HALO), :]
            slot += 1


def rows_to_message(raw, message, at_start):
    now, before, speed = raw
    first, second, third = (jnp.where(at_start, k, 2 * HALO - 1 - k) for k in range(3))
    cells = slice(LEFT - HALO, LEFT - HALO + WIDE)
    beyond = speed[second, cells, :] * later_row(now, before, speed, third, LEFT - HALO, WIDE)
    values = (
        now[first, cells, :],
        now[second, cells, :] - beyond,
        before[first, cells, :] - speed[first, cells, :] * beyond,
        later_row(now, before, speed, second, LEFT - HALO, WIDE),
        speed[first, cells, :],
        speed[second, cells, :],
    )
    for value, at, reach in zip(values, PLACES, REACHES):
        message[at : at + COLS + 2 * reach] = value[HALO - reach : HALO + COLS + reach]


def message_to_rows(padded, message, at_start, place=0):
    for slot, (at, reach) in enumerate(zip(PLACES, REACHES)):
        row = HALO + jnp.where(at_start, -1 - slot % 2, ROWS + slot % 2)
        width = COLS + 2 * reach
        padded[slot // 2][row, LEFT - reach : LEFT + COLS + reach, :] = message[pl.ds(place + at, width), :]


def outer_kernel(pressure, earlier, speed, message, tiles, sems):
    first_core = lax.axis_index("core") == 0
    first = pl.multiple_of(jnp.where(first_core, 0, COLS - TILE), TILE)
    copies = [
        pltpu.make_async_copy(source.at[:, pl.ds(first, TILE), :], tiles.at[i], sems.at[i])
        for i, source in enumerate((pressure, earlier, speed))
    ]
    for copy in copies:
        copy.start()
    slot = 0
    for i, depth in enumerate(DEPTHS):
        copies[i].wait()
        cells = tiles.at[i].reshape(ROWS * TILE, MEMBERS)
        start = jnp.where(first_core, 0, TILE - depth)
        for k in range(depth):
            message[pl.ds(slot * ROWS, ROWS), :] = cells[pl.ds(start + k, ROWS, stride=TILE), :]
            slot += 1


def load_kernel(pressure, earlier, speed, *refs):
    padded, raw, inner = refs[:3], refs[3:6], refs[6]
    for source, target, ends in zip((pressure, earlier, speed), padded, raw):
        for k in range(HALO):
            ends[k, LEFT : LEFT + COLS, :] = source[k]
            ends[HALO + k, LEFT : LEFT + COLS, :] = source[ROWS - HALO + k]

        def some(i, _, source=source, target=target):
            for k in range(4):
                target[HALO + 4 * i + k, LEFT : LEFT + COLS, :] = source[4 * i + k]
            return 0

        lax.fori_loop(0, ROWS // 4, some, 0)
    columns_to_message(padded, inner, lax.axis_index("core") != 0)


def columns_kernel(*refs):
    outer, inner = refs[6:8]
    padded, raw, (odd, even) = refs[8:11], refs[11:14], refs[14:16]
    first_core = lax.axis_index("core") == 0
    message_to_columns(padded, raw, outer, first_core)
    message_to_columns(padded, raw, inner, jnp.logical_not(first_core), jnp.where(first_core, DEEP, 0))
    odd_x = lax.axis_index(X) % 2 == 1
    rows_to_message(raw, odd, jnp.logical_not(odd_x))
    rows_to_message(raw, even, odd_x)
    for row in (HALO - 3, HALO + ROWS + 2):
        padded[1][row] = jnp.zeros((PITCH, MEMBERS), jnp.float32)


def later_row(source, before, speed, row, first, width):
    cells = slice(first, first + width)
    middle = source[row, cells, :]
    spread = source[row - 1, cells, :] + source[row + 1, cells, :]
    spread += source[row, first - 1 : first - 1 + width, :]
    spread += source[row, first + 1 : first + 1 + width, :]
    spread -= 4.0 * middle
    return 2.0 * middle - before[row, cells, :] + speed[row, cells, :] * spread


def set_later_row(source, before, speed, row, first=-HALO, width=WIDE):
    cells = slice(LEFT + first, LEFT + first + width)
    before[row, cells, :] = later_row(source, before, speed, row, LEFT + first, width)


def own_steps(padded, end, sums, inside):
    now, before, speed = padded
    for step in range(1, STEPS):

        def pair(i, _, now=now, before=before, step=step):
            for k in range(2):
                row = HALO + step + 2 * i + k
                set_later_row(now, before, speed, row, step, COLS - 2 * step)
            return 0

        lax.fori_loop(0, (ROWS - 2 * step) // 2, pair, 0)
        now, before = before, now
    cells = slice(STEPS, COLS - STEPS)

    def last(i, total):
        for k in range(2):
            row = STEPS + 2 * i + k
            value = later_row(now, before, speed, row + HALO, LEFT + STEPS, COLS - 2 * STEPS)
            end[row, cells, :] = value
            total = total + value
            sums[row, cells, :] = total * SCALE
        return total

    zero = jnp.zeros((COLS - 2 * STEPS, MEMBERS), jnp.float32)
    inside[cells, :] = lax.fori_loop(0, INSIDE // 2, last, zero)


def first_core_kernel(_p, _e, _s, _message, *refs):
    @pl.when(lax.axis_index("core") == 0)
    def _():
        own_steps(refs[:3], *refs[4:])


def second_core_kernel(_p, _e, _s, _end, _sums, _inside, _message, *refs):
    @pl.when(lax.axis_index("core") != 0)
    def _():
        own_steps(refs[:3], *refs[3:])


def edges_kernel(_p, _e, _s, odd, even, _end, _sums, _inside, *refs):
    padded, (end, sums, inside, offsets, copies) = refs[:3], refs[3:]
    now, before, speed = padded
    for step in range(1, STEPS):
        for row in range(step, ROWS - step):
            for first in (step - STEPS, COLS - step):
                set_later_row(now, before, speed, row + HALO, first, STEPS)
        now, before = before, now
    for first in (0, COLS - STEPS):
        cells = slice(first, first + STEPS)
        total = jnp.zeros((STEPS, MEMBERS), jnp.float32)
        for row in range(STEPS, ROWS - STEPS):
            value = later_row(now, before, speed, row + HALO, LEFT + first, STEPS)
            end[row, cells, :] = value
            total = total + value
            sums[row, cells, :] = total * SCALE
        inside[cells, :] = total

    odd_x = lax.axis_index(X) % 2 == 1
    message_to_rows(padded, odd, jnp.logical_not(odd_x))
    message_to_rows(padded, even, odd_x, jnp.where(odd_x, 0, ROW_CELLS))
    now, before, speed = padded
    for first, count in ((-1, 2), (-2, 4), (-1, 4)):
        for k in range(count):
            set_later_row(now, before, speed, HALO + first + k)
            set_later_row(now, before, speed, HALO + ROWS - 1 - first - k)
        now, before = before, now
    total = jnp.zeros((COLS, MEMBERS), jnp.float32)
    for side in range(2):
        here = jnp.zeros((COLS, MEMBERS), jnp.float32)
        for k in range(STEPS):
            row = side * (ROWS - STEPS) + k
            value = later_row(now, before, speed, row + HALO, LEFT, COLS)
            end[row] = value
            here = here + value
            sums[row] = here * SCALE
        total = total + here
        if side == 0:
            offsets[0] = total * SCALE
            total = total + inside[...]
            offsets[1] = total * SCALE
    for k in range(copies.shape[0]):
        copies[k] = total


def middle_kernel(row, copies, before):
    here = lax.axis_index(X)
    total = jnp.zeros((COLS, MEMBERS), jnp.float32)
    for k in range(row.shape[0]):
        before[...] = jnp.where(k == here, total, before[...])
        total = total + row[k]
    for k in range(copies.shape[0]):
        copies[k] = total


def final_kernel(rows, before, sums, offsets, end, potential_out, end_out, potential, sems):
    copies = [pltpu.make_async_copy(end, end_out, sems.at[FINAL_PIECES])]
    copies[0].start()
    here = lax.axis_index("y")
    total = before[...]
    for k in range(rows.shape[0]):
        total = total + jnp.where(k < here, rows[k], 0.0)
    total = total * SCALE
    inner = total + offsets[0]
    upper = total + offsets[1]
    piece = ROWS // FINAL_PIECES
    for part in range(FINAL_PIECES):
        for row in range(part * piece, (part + 1) * piece):
            below = total if row < STEPS else inner if row < ROWS - STEPS else upper
            potential[row] = sums[row] + below
        place = pl.ds(part * piece, piece)
        copy = pltpu.make_async_copy(potential.at[place], potential_out.at[place], sems.at[part])
        copy.start()
        copies.append(copy)
    for copy in copies:
        copy.wait()


def on_device(pressure, earlier, speed_square):
    args = [pltpu.with_memory_space_constraint(a, pltpu.HBM) for a in (pressure, earlier, speed_square)]
    outer = call(
        outer_kernel,
        in_vmem(DEEP * ROWS),
        "outer",
        args,
        [HBM] * 3,
        VMEM,
        [in_vmem(3, ROWS, TILE), pltpu.SemaphoreType.DMA((3,))],
    )
    chips, ys, xs = (lax.axis_size(name) for name in ("z", "y", X))
    swap = lambda pairs: pairs + [(b, a) for a, b in pairs]
    outer = lax.ppermute(outer, LON, swap([(2 * z + 1, 2 * z + 2) for z in range(chips - 1)]))
    *padded, inner = call(
        load_kernel,
        [PADDED] * 3 + [RAW] * 3 + [in_vmem(DEEP * ROWS)],
        "load",
        [pltpu.with_memory_space_constraint(a, pltpu.VMEM) for a in (pressure, earlier, speed_square)],
        [VMEM] * 3,
        [VMEM] * 7,
    )
    padded, raw = padded[:3], padded[3:]
    same = {0: 0, 1: 1, 2: 2}
    *padded, inner, end, sums, inside = call(
        first_core_kernel,
        [PADDED] * 3 + [in_vmem(DEEP * ROWS)] + [in_vmem(ROWS, COLS)] * 2 + [in_vmem(COLS)],
        "own0",
        (*padded, inner),
        [VMEM] * 4,
        [VMEM] * 7,
        aliases={**same, 3: 3},
    )
    inner = lax.all_gather(inner, "core", axis=0, tiled=True)
    *padded, end, sums, inside = call(
        second_core_kernel,
        [PADDED] * 3 + [in_vmem(ROWS, COLS)] * 2 + [in_vmem(COLS)],
        "own1",
        (*padded, end, sums, inside, inner),
        [VMEM] * 7,
        [VMEM] * 6,
        aliases={k: k for k in range(6)},
        flops=10**8,
    )
    *padded, odd, even = call(
        columns_kernel,
        [PADDED] * 3 + [RAW] * 3 + [in_vmem(ROW_CELLS)] * 2,
        "columns",
        (*padded, *raw, outer, inner),
        [VMEM] * 8,
        [VMEM] * 8,
        aliases={k: k for k in range(6)},
    )
    padded = padded[:3]
    blocks = ys * xs
    odd = lax.ppermute(odd, LAT, swap([(i, i + 1) for i in range(1, blocks - 1, 2)]))
    even = lax.all_gather(even, "xl", axis=0, tiled=True)
    *_, end, sums, _, offsets, copies = call(
        edges_kernel,
        [PADDED] * 3 + [in_vmem(ROWS, COLS)] * 2 + [in_vmem(COLS), in_vmem(2, COLS), in_vmem(xs, COLS)],
        "edges",
        (*padded, odd, even, end, sums, inside),
        [VMEM] * 8,
        [VMEM] * 8,
        aliases={**same, 5: 3, 6: 4, 7: 5},
    )
    row = lax.all_to_all(copies, X, 0, 0, tiled=True)
    copies, before = call(
        middle_kernel,
        [in_vmem(ys, COLS), in_vmem(COLS)],
        "middle",
        (row,),
        [VMEM],
        [VMEM] * 2,
    )
    rows = lax.all_to_all(copies, "y", 0, 0, tiled=True)
    return call(
        final_kernel,
        [WHOLE] * 2,
        "final",
        (rows, before, sums, offsets, end),
        [VMEM] * 5,
        [HBM] * 2,
        [in_vmem(ROWS, COLS), pltpu.SemaphoreType.DMA((FINAL_PIECES + 1,))],
    )


def solution(mesh):
    fine = Mesh(mesh.devices.reshape(8, 2, 2, 8, 2), ("y", *X, "z", "core"))
    spec = P(LAT, LON, None)
    return jax.shard_map(
        on_device, mesh=fine, in_specs=(spec,) * 3, out_specs=(spec,) * 2, check_vma=False
    )
```

time: 47.2 us -> 46.6 us (0.987)
  blocking collectives: 31.1 us -> 39 us
  starting transfers between devices: 8.72 us -> 2.59 us
  waiting for transfers between devices: 1.98 us -> 0.01 us
    all_gather x0 -> x1, blocking collectives: none -> 8.47 us  [on_device(): even = lax.all_gather(even, 'xl', axis=0, tiled=True)]
    ppermute x1 -> x0, starting transfers between devices: 6.13 us -> none  [on_device(): lax.ppermute(even, LAT, swap([(i, i + 1) for i in range(0, blocks, 2)]))]
    ppermute x1 -> x0, waiting for transfers between devices: 1.97 us -> none  [on_device(): lax.ppermute(even, LAT, swap([(i, i + 1) for i in range(0, blocks, 2)]))]
    all_gather x1, blocking collectives: 5.36 us -> 4.46 us  [on_device(): inner = lax.all_gather(inner, 'core', axis=0, tiled=True)]
    pallas_call x7 -> x8, Pallas kernels: 4.38 us -> 3.97 us  [call(): pl.pallas_call(kernel, out_shape=outs, in_specs=specs, out_specs=out_spec...]
  transfers between devices with their start and end apart: 3 -> 2, of which waited for: 1 -> 0; matrix products, arithmetic and copies ran while one was open for 0% -> 0% of each run, Pallas kernels for 4% -> 2%
where the time goes in v8:
time: 46.6 us; the launch traced here: 46.3 us
  blocking collectives  39 us (84%)
  Pallas kernels  3.97 us (9%)
  starting transfers between devices  2.59 us (6%)
  between operations  0.74 us (2%)
    all_to_all x1, blocking collectives, on_device(): rows = lax.all_to_all(copies, 'y', 0, 0, tiled=True)  15.8 us
    all_to_all x1, blocking collectives, on_device(): row = lax.all_to_all(copies, X, 0, 0, tiled=True)  10.3 us
    all_gather x1, blocking collectives, on_device(): even = lax.all_gather(even, 'xl', axis=0, tiled=True)  8.47 us
    all_gather x1, blocking collectives, on_device(): inner = lax.all_gather(inner, 'core', axis=0, tiled=True)  4.46 us
    pallas_call x8, Pallas kernels, call(): pl.pallas_call(kernel, out_shape=outs, in_specs=specs, out_specs=out_spec...  3.97 us
    ppermute x1, starting transfers between devices, on_device(): lax.ppermute(outer, LON, swap([(2 * z + 1, 2 * z + 2) for z in range(chip...  1.92 us
  transfers between devices with their start and end apart: 2, of which 0 were waited for; matrix products, arithmetic and copies ran while one was open for 0% of the time, Pallas kernels for 2%

profile of v8, /device:TPU:192, one launch (start us, length us, event | category | flops | bytes accessed | tf_op | source)
XLA Modules:
  0.0 46.3 jit_solution(1132529981294518321)
XLA Ops:
  0.6 0.0 copy-start
  0.6 0.0 copy-start.1
  0.6 0.0 copy-start.2
  0.7 1.2 %outer.1 = f32[320,128]{1,0:T(8,128)S(1)} custom-call(f32[32,32,128]{2,1,0:T(8,128)} %pressure.3, f32[32,32,128]{2,1,0:T(8,128)} %earlier.3, f32[32,32,128]{2,1,0:T(8,128)} %speed.3), custom_call_target="tpu_custom_call" | custom-call | flops 100000 | tf_op jit(solution)/shard_map/outer/pallas_call | solution.py:44
  1.9 1.9 %collective-permute-start = (f32[320,128]{1,0:T(8,128)S(1)}, f32[320,128]{1,0:T(8,128)S(1)}, u32[]{:S(2)}, u32[]{:S(2)}) collective-permute-start(f32[320,128]{1,0:T(8,128)S(1)} %outer.1), channel_id=1, source_target_pairs={{1,2},{3,4},{5,6},{7,8},{9,10},{11,12},{13,14},{2,1},{4,3},{6,5},{... | collective-permute-start | bytes 491528 | tf_op jit(solution)/shard_map/ppermute | solution.py:299
  3.8 0.0 copy-done
  3.8 0.0 copy-done.1
  3.8 0.0 copy-done.2
  3.8 0.2 load.1
  4.0 0.9 %own0.1 = (f32[40,56,128]{2,1,0:T(8,128)S(1)}, f32[40,56,128]{2,1,0:T(8,128)S(1)}, f32[40,56,128]{2,1,0:T(8,128)S(1)}, f32[320,128]{1,0:T(8,128)S(1)}, f32[32,32...) custom-call(f32[40,56,128]{2,1,0:T(8,128)S(1)} %get-tuple-element.33, ...), custom_call_target="tpu_custom_call", output_to_operand_aliasing={{0}: (0, {}), {1}: (1, {}), {2}: (2, {}), {3}: (3, {})} | custom-call | flops 100000 | tf_op jit(solution)/shard_map/own0/pallas_call | solution.py:44
  5.0 4.5 %all_gather.6._message.refs_7_ = f32[640,128]{1,0:T(8,128)S(1)} all-gather(f32[320,128]{1,0:T(8,128)S(1)} %get-tuple-element.43), channel_id=1, replica_groups=mesh['y'=8,'xh'=2,'xl'=2,'z'=8,'core'=2] {'core'}, dimensions={0}, use_global_device_ids=true | all-gather | bytes 491520 | tf_op jit(solution)/shard_map/all_gather | solution.py:319
  9.4 0.0 collective-permute-done.refs_6_
  9.4 0.1 columns.1
  9.6 0.7 %collective-permute-start.1 = (f32[216,128]{1,0:T(8,128)S(1)}, f32[216,128]{1,0:T(8,128)S(1)}, u32[]{:S(2)}, u32[]{:S(2)}) collective-permute-start(f32[216,128]{1,0:T(8,128)S(1)} %get-tuple-element.53), channel_id=1, source_target_pairs={{16,32},{48,64},{80,96},{112,128},{144,160},{176,192},{208,224},{2... | collective-permute-start | bytes 331784 | tf_op jit(solution)/shard_map/ppermute | solution.py:341
  10.2 8.5 %all_gather.7.even = f32[432,128]{1,0:T(8,128)S(1)} all-gather(f32[216,128]{1,0:T(8,128)S(1)} %get-tuple-element.54), channel_id=1, replica_groups=mesh['y'=8,'xh'=2,'xl'=2,'z'=8,'core'=2] {'xl'}, dimensions={0}, use_global_device_ids=true | all-gather | bytes 331776 | tf_op jit(solution)/shard_map/all_gather | solution.py:342
  18.7 0.0 collective-permute-done.1.odd
  18.7 0.5 %edges.1 = (f32[40,56,128]{2,1,0:T(8,128)S(1)}, f32[40,56,128]{2,1,0:T(8,128)S(1)}, f32[40,56,128]{2,1,0:T(8,128)S(1)}, f32[32,32,128]{2,1,0:T(8,128)S(1)}, f32[...) custom-call(f32[40,56,128]{2,1,0:T(8,128)S(1)} %get-tuple-element.50, ...), custom_call_target="tpu_custom_call", output_to_operand_aliasing={{0}: (0, {}), {1}: (1, {}), {2}: (2, {}), {3}: (5, {}), {4}... | custom-call | flops 100000 | tf_op jit(solution)/shard_map/edges/pallas_call | solution.py:44
  19.2 10.3 %all_to_all.10.row = f32[4,32,128]{2,1,0:T(8,128)S(1)} all-to-all(f32[4,32,128]{2,1,0:T(8,128)S(1)} %get-tuple-element.58), channel_id=1, replica_groups=mesh['y'=8,'xh'=2,'xl'=2,'z'=8,'core'=2] {'xh','xl'}, dimensions={0} | all-to-all | bytes 131072 | tf_op jit(solution)/shard_map/all_to_all | solution.py:352
  29.5 15.8 %all_to_all.11.rows = f32[8,32,128]{2,1,0:T(8,128)S(1)} all-to-all(f32[8,32,128]{2,1,0:T(8,128)S(1)} %get-tuple-element.59), channel_id=1, replica_groups=mesh['y'=8,'xh'=2,'xl'=2,'z'=8,'core'=2] {'y'}, dimensions={0} | all-to-all | bytes 262144 | tf_op jit(solution)/shard_map/all_to_all | solution.py:361
  45.3 1.0 %final.1 = (f32[32,32,128]{2,1,0:T(8,128)}, f32[32,32,128]{2,1,0:T(8,128)}) custom-call(f32[8,32,128]{2,1,0:T(8,128)S(1)} %all_to_all.11.rows, f32[32,128]{1,0:T(8,128)S(1)} %get-tuple-element.60.before, f32[32,32,128]{2,1,0:T(8,128)S(1)} %get-tuple-element.61.sums, f32[2,32,128]{2,1,0:T(8,128)S(1)} %get-tuple-element.62.offsets, ...), custom_call_target="tpu_custom_call" | custom-call | flops 100000 | tf_op jit(solution)/shard_map/final/pallas_call | solution.py:44
  (2 shorter events, 0.0 us)
Async XLA Ops:
  0.6 3.2 %copy-start = (f32[32,32,128]{2,1,0:T(8,128)S(1)}, f32[32,32,128]{2,1,0:T(8,128)}, u32[]{:S(2)}) copy-start(f32[32,32,128]{2,1,0:T(8,128)} %pressure.3) | copy-start | bytes 1572868
  0.6 3.2 %copy-start.1 = (f32[32,32,128]{2,1,0:T(8,128)S(1)}, f32[32,32,128]{2,1,0:T(8,128)}, u32[]{:S(2)}) copy-start(f32[32,32,128]{2,1,0:T(8,128)} %earlier.3) | copy-start | bytes 1572868
  0.6 3.2 %copy-start.2 = (f32[32,32,128]{2,1,0:T(8,128)S(1)}, f32[32,32,128]{2,1,0:T(8,128)}, u32[]{:S(2)}) copy-start(f32[32,32,128]{2,1,0:T(8,128)} %speed.3) | copy-start | bytes 1572868
  1.9 7.6 %collective-permute-start = (f32[320,128]{1,0:T(8,128)S(1)}, f32[320,128]{1,0:T(8,128)S(1)}, u32[]{:S(2)}, u32[]{:S(2)}) collective-permute-start(f32[320,128]{1,0:T(8,128)S(1)} %outer.1), channel_id=1, source_target_pairs={{1,2},{3,4},{5,6},{7,8},{9,10},{11,12},{13,14},{2,1},{4,3},{6,5},{... | collective-permute-start | bytes 491528 | tf_op jit(solution)/shard_map/ppermute | solution.py:299
  9.6 9.2 %collective-permute-start.1 = (f32[216,128]{1,0:T(8,128)S(1)}, f32[216,128]{1,0:T(8,128)S(1)}, u32[]{:S(2)}, u32[]{:S(2)}) collective-permute-start(f32[216,128]{1,0:T(8,128)S(1)} %get-tuple-element.53), channel_id=1, source_target_pairs={{16,32},{48,64},{80,96},{112,128},{144,160},{176,192},{208,224},{2... | collective-permute-start | bytes 331784 | tf_op jit(solution)/shard_map/ppermute | solution.py:341

commit v9 on v8

--- a/solution.py
+++ b/solution.py
@@ -29,7 +29,7 @@
 VMEM = pl.BlockSpec(memory_space=pltpu.VMEM)
 WHOLE = pltpu.HBM((ROWS, COLS, MEMBERS), jnp.float32)
 PADDED = pltpu.VMEM((TALL, PITCH, MEMBERS), jnp.float32)
-RAW = pltpu.VMEM((2 * HALO, PITCH, MEMBERS), jnp.float32)
+RAW = pltpu.VMEM((3 * HALO, PITCH, MEMBERS), jnp.float32)
 
 
 def in_vmem(*shape):
@@ -73,9 +73,11 @@
         for k in range(depth):
             at = slot * ROWS
             flat(ref)[pl.ds(cell(0, first + k), ROWS, stride=PITCH), :] = message[pl.ds(at, ROWS), :]
-            for row, source in ((0, at), (HALO, at + ROWS - HALO)):
+            first_rows = message[pl.ds(at, 2 * HALO), :][:HALO]
+            last_rows = message[pl.ds(at + ROWS - 2 * HALO, 2 * HALO), :][HALO:]
+            for row, values in ((0, first_rows), (HALO, last_rows)):
                 place = pl.ds(row * PITCH + LEFT + first + k, HALO, stride=PITCH)
-                flat(ends)[place, :] = message[pl.ds(source, HALO), :]
+                flat(ends)[place, :] = values
             slot += 1
 
 
@@ -107,7 +109,7 @@
     first_core = lax.axis_index("core") == 0
     first = pl.multiple_of(jnp.where(first_core, 0, COLS - TILE), TILE)
     copies = [
-        pltpu.make_async_copy(source.at[:, pl.ds(first, TILE), :], tiles.at[i], sems.at[i])
+        pltpu.make_async_copy(source.at[:, pl.ds(first, TILE), :], tiles.at[i, pl.ds(0, ROWS)], sems.at[i])
         for i, source in enumerate((pressure, earlier, speed))
     ]
     for copy in copies:
@@ -115,7 +117,7 @@
     slot = 0
     for i, depth in enumerate(DEPTHS):
         copies[i].wait()
-        cells = tiles.at[i].reshape(ROWS * TILE, MEMBERS)
+        cells = tiles.at[i].reshape((ROWS + 1) * TILE, MEMBERS)
         start = jnp.where(first_core, 0, TILE - depth)
         for k in range(depth):
             message[pl.ds(slot * ROWS, ROWS), :] = cells[pl.ds(start + k, ROWS, stride=TILE), :]
@@ -244,7 +246,7 @@
         total = total + here
         if side == 0:
             offsets[0] = total * SCALE
-            total = total + inside[...]
+            total = total + inside[:COLS]
             offsets[1] = total * SCALE
     for k in range(copies.shape[0]):
         copies[k] = total
@@ -292,7 +294,7 @@
         args,
         [HBM] * 3,
         VMEM,
-        [in_vmem(3, ROWS, TILE), pltpu.SemaphoreType.DMA((3,))],
+        [in_vmem(3, ROWS + 1, TILE), pltpu.SemaphoreType.DMA((3,))],
     )
     chips, ys, xs = (lax.axis_size(name) for name in ("z", "y", X))
     swap = lambda pairs: pairs + [(b, a) for a, b in pairs]
@@ -309,7 +311,7 @@
     same = {0: 0, 1: 1, 2: 2}
     *padded, inner, end, sums, inside = call(
         first_core_kernel,
-        [PADDED] * 3 + [in_vmem(DEEP * ROWS)] + [in_vmem(ROWS, COLS)] * 2 + [in_vmem(COLS)],
+        [PADDED] * 3 + [in_vmem(DEEP * ROWS)] + [in_vmem(ROWS, COLS)] * 2 + [in_vmem(COLS + 8)],
         "own0",
         (*padded, inner),
         [VMEM] * 4,
@@ -319,7 +321,7 @@
     inner = lax.all_gather(inner, "core", axis=0, tiled=True)
     *padded, end, sums, inside = call(
         second_core_kernel,
-        [PADDED] * 3 + [in_vmem(ROWS, COLS)] * 2 + [in_vmem(COLS)],
+        [PADDED] * 3 + [in_vmem(ROWS, COLS)] * 2 + [in_vmem(COLS + 8)],
         "own1",
         (*padded, end, sums, inside, inner),
         [VMEM] * 7,
@@ -342,7 +344,7 @@
     even = lax.all_gather(even, "xl", axis=0, tiled=True)
     *_, end, sums, _, offsets, copies = call(
         edges_kernel,
-        [PADDED] * 3 + [in_vmem(ROWS, COLS)] * 2 + [in_vmem(COLS), in_vmem(2, COLS), in_vmem(xs, COLS)],
+        [PADDED] * 3 + [in_vmem(ROWS, COLS)] * 2 + [in_vmem(COLS + 8), in_vmem(2, COLS), in_vmem(xs, COLS)],
         "edges",
         (*padded, odd, even, end, sums, inside),
         [VMEM] * 8,

time: 46.6 us -> 46.5 us (level)
  no operation moved by 1% of the time
where the time goes in v9:
time: 46.5 us; the launch traced here: 46.3 us
  blocking collectives  39 us (84%)
  Pallas kernels  3.96 us (9%)
  starting transfers between devices  2.59 us (6%)
  between operations  0.74 us (2%)
    all_to_all x1, blocking collectives, on_device(): rows = lax.all_to_all(copies, 'y', 0, 0, tiled=True)  15.8 us
    all_to_all x1, blocking collectives, on_device(): row = lax.all_to_all(copies, X, 0, 0, tiled=True)  10.3 us
    all_gather x1, blocking collectives, on_device(): even = lax.all_gather(even, 'xl', axis=0, tiled=True)  8.47 us
    all_gather x1, blocking collectives, on_device(): inner = lax.all_gather(inner, 'core', axis=0, tiled=True)  4.46 us
    pallas_call x8, Pallas kernels, call(): pl.pallas_call(kernel, out_shape=outs, in_specs=specs, out_specs=out_spec...  3.96 us
    ppermute x1, starting transfers between devices, on_device(): lax.ppermute(outer, LON, swap([(2 * z + 1, 2 * z + 2) for z in range(chip...  1.92 us
  transfers between devices with their start and end apart: 2, of which 0 were waited for; matrix products, arithmetic and copies ran while one was open for 0% of the time, Pallas kernels for 2%

profile of v9, /device:TPU:192, one launch (start us, length us, event | category | flops | bytes accessed | tf_op | source)
XLA Modules:
  0.0 46.3 jit_solution(3488181858899080399)
XLA Ops:
  0.6 0.0 copy-start.2
  0.6 0.0 copy-start.1
  0.6 0.0 copy-start
  0.7 1.2 %outer.1 = f32[320,128]{1,0:T(8,128)S(1)} custom-call(f32[32,32,128]{2,1,0:T(8,128)} %pressure.3, f32[32,32,128]{2,1,0:T(8,128)} %earlier.3, f32[32,32,128]{2,1,0:T(8,128)} %speed.3), custom_call_target="tpu_custom_call" | custom-call | flops 100000 | tf_op jit(solution)/shard_map/outer/pallas_call | solution.py:44
  1.9 1.9 %collective-permute-start = (f32[320,128]{1,0:T(8,128)S(1)}, f32[320,128]{1,0:T(8,128)S(1)}, u32[]{:S(2)}, u32[]{:S(2)}) collective-permute-start(f32[320,128]{1,0:T(8,128)S(1)} %outer.1), channel_id=1, source_target_pairs={{1,2},{3,4},{5,6},{7,8},{9,10},{11,12},{13,14},{2,1},{4,3},{6,5},{... | collective-permute-start | bytes 491528 | tf_op jit(solution)/shard_map/ppermute | solution.py:301
  3.8 0.0 copy-done.2
  3.8 0.0 copy-done.1
  3.8 0.0 copy-done
  3.8 0.2 load.1
  4.0 0.9 %own0.1 = (f32[40,56,128]{2,1,0:T(8,128)S(1)}, f32[40,56,128]{2,1,0:T(8,128)S(1)}, f32[40,56,128]{2,1,0:T(8,128)S(1)}, f32[320,128]{1,0:T(8,128)S(1)}, f32[32,32...) custom-call(f32[40,56,128]{2,1,0:T(8,128)S(1)} %get-tuple-element.33, ...), custom_call_target="tpu_custom_call", output_to_operand_aliasing={{0}: (0, {}), {1}: (1, {}), {2}: (2, {}), {3}: (3, {})} | custom-call | flops 100000 | tf_op jit(solution)/shard_map/own0/pallas_call | solution.py:44
  5.0 4.5 %all_gather.6._message.refs_7_ = f32[640,128]{1,0:T(8,128)S(1)} all-gather(f32[320,128]{1,0:T(8,128)S(1)} %get-tuple-element.43), channel_id=1, replica_groups=mesh['y'=8,'xh'=2,'xl'=2,'z'=8,'core'=2] {'core'}, dimensions={0}, use_global_device_ids=true | all-gather | bytes 491520 | tf_op jit(solution)/shard_map/all_gather | solution.py:321
  9.4 0.0 collective-permute-done.refs_6_
  9.4 0.1 columns.1
  9.6 0.7 %collective-permute-start.1 = (f32[216,128]{1,0:T(8,128)S(1)}, f32[216,128]{1,0:T(8,128)S(1)}, u32[]{:S(2)}, u32[]{:S(2)}) collective-permute-start(f32[216,128]{1,0:T(8,128)S(1)} %get-tuple-element.53), channel_id=1, source_target_pairs={{16,32},{48,64},{80,96},{112,128},{144,160},{176,192},{208,224},{2... | collective-permute-start | bytes 331784 | tf_op jit(solution)/shard_map/ppermute | solution.py:343
  10.2 8.5 %all_gather.7.even = f32[432,128]{1,0:T(8,128)S(1)} all-gather(f32[216,128]{1,0:T(8,128)S(1)} %get-tuple-element.54), channel_id=1, replica_groups=mesh['y'=8,'xh'=2,'xl'=2,'z'=8,'core'=2] {'xl'}, dimensions={0}, use_global_device_ids=true | all-gather | bytes 331776 | tf_op jit(solution)/shard_map/all_gather | solution.py:344
  18.7 0.0 collective-permute-done.1.odd
  18.7 0.5 %edges.1 = (f32[40,56,128]{2,1,0:T(8,128)S(1)}, f32[40,56,128]{2,1,0:T(8,128)S(1)}, f32[40,56,128]{2,1,0:T(8,128)S(1)}, f32[32,32,128]{2,1,0:T(8,128)S(1)}, f32[...) custom-call(f32[40,56,128]{2,1,0:T(8,128)S(1)} %get-tuple-element.50, ...), custom_call_target="tpu_custom_call", output_to_operand_aliasing={{0}: (0, {}), {1}: (1, {}), {2}: (2, {}), {3}: (5, {}), {4}... | custom-call | flops 100000 | tf_op jit(solution)/shard_map/edges/pallas_call | solution.py:44
  19.2 10.3 %all_to_all.10.row = f32[4,32,128]{2,1,0:T(8,128)S(1)} all-to-all(f32[4,32,128]{2,1,0:T(8,128)S(1)} %get-tuple-element.58), channel_id=1, replica_groups=mesh['y'=8,'xh'=2,'xl'=2,'z'=8,'core'=2] {'xh','xl'}, dimensions={0} | all-to-all | bytes 131072 | tf_op jit(solution)/shard_map/all_to_all | solution.py:354
  29.5 15.8 %all_to_all.11.rows = f32[8,32,128]{2,1,0:T(8,128)S(1)} all-to-all(f32[8,32,128]{2,1,0:T(8,128)S(1)} %get-tuple-element.59), channel_id=1, replica_groups=mesh['y'=8,'xh'=2,'xl'=2,'z'=8,'core'=2] {'y'}, dimensions={0} | all-to-all | bytes 262144 | tf_op jit(solution)/shard_map/all_to_all | solution.py:363
  45.3 1.0 %final.1 = (f32[32,32,128]{2,1,0:T(8,128)}, f32[32,32,128]{2,1,0:T(8,128)}) custom-call(f32[8,32,128]{2,1,0:T(8,128)S(1)} %all_to_all.11.rows, f32[32,128]{1,0:T(8,128)S(1)} %get-tuple-element.60.before, f32[32,32,128]{2,1,0:T(8,128)S(1)} %get-tuple-element.61.sums, f32[2,32,128]{2,1,0:T(8,128)S(1)} %get-tuple-element.62.offsets, ...), custom_call_target="tpu_custom_call" | custom-call | flops 100000 | tf_op jit(solution)/shard_map/final/pallas_call | solution.py:44
  (2 shorter events, 0.0 us)
Async XLA Ops:
  0.6 3.2 %copy-start.2 = (f32[32,32,128]{2,1,0:T(8,128)S(1)}, f32[32,32,128]{2,1,0:T(8,128)}, u32[]{:S(2)}) copy-start(f32[32,32,128]{2,1,0:T(8,128)} %speed.3) | copy-start | bytes 1572868
  0.6 3.2 %copy-start.1 = (f32[32,32,128]{2,1,0:T(8,128)S(1)}, f32[32,32,128]{2,1,0:T(8,128)}, u32[]{:S(2)}) copy-start(f32[32,32,128]{2,1,0:T(8,128)} %earlier.3) | copy-start | bytes 1572868
  0.6 3.2 %copy-start = (f32[32,32,128]{2,1,0:T(8,128)S(1)}, f32[32,32,128]{2,1,0:T(8,128)}, u32[]{:S(2)}) copy-start(f32[32,32,128]{2,1,0:T(8,128)} %pressure.3) | copy-start | bytes 1572868
  1.9 7.6 %collective-permute-start = (f32[320,128]{1,0:T(8,128)S(1)}, f32[320,128]{1,0:T(8,128)S(1)}, u32[]{:S(2)}, u32[]{:S(2)}) collective-permute-start(f32[320,128]{1,0:T(8,128)S(1)} %outer.1), channel_id=1, source_target_pairs={{1,2},{3,4},{5,6},{7,8},{9,10},{11,12},{13,14},{2,1},{4,3},{6,5},{... | collective-permute-start | bytes 491528 | tf_op jit(solution)/shard_map/ppermute | solution.py:301
  9.6 9.2 %collective-permute-start.1 = (f32[216,128]{1,0:T(8,128)S(1)}, f32[216,128]{1,0:T(8,128)S(1)}, u32[]{:S(2)}, u32[]{:S(2)}) collective-permute-start(f32[216,128]{1,0:T(8,128)S(1)} %get-tuple-element.53), channel_id=1, source_target_pairs={{16,32},{48,64},{80,96},{112,128},{144,160},{176,192},{208,224},{2... | collective-permute-start | bytes 331784 | tf_op jit(solution)/shard_map/ppermute | solution.py:343
